TPU v7x, 256 devices: a whole 4x4x8 slice. The times are simulated.
256 devices in a mesh: sky: 64 (over x_hi, y, z), band: 4 (over x_lo, core).
Axes of the slice: x: 4 (x_hi: 2, x_lo: 2; x = x_hi * 2 + x_lo), y: 4, z: 8, core: 2. Of those that a mesh axis runs over, the one named last changes fastest.
Arguments:
- magnitudes: float32 [4, 8, 131072], P('band', None, 'sky'), may hold values from -7 to 7
- weights: float32 [4, 8, 131072], P('band', None, 'sky'), may hold values from 0.25 to 4
- slots: int32 [4, 8, 131072], P('band', None, 'sky'), may hold values from 0 to 31, as said below
- block_fields: int32 [512, 32], P('sky'), may hold values from 0 to 4096, as said below
- owner: int32 [4096], replicated, may hold values from 0 to 63, as said below
- colors: int32 [4096], replicated, may hold values from 0 to 7
- color_terms: float32 [4, 4], replicated, may hold values from -0.25 to 0.25
Outputs:
- zero_points: float32 [4, 4096], P('band', 'sky')
- star_mags: float32 [4, 131072], P('band', 'sky')
- misfit: float32 [4, 4], P(None, 'band')
Inputs may be any that keep to these rules, and one draw needn't show every extreme that they name: `block_fields`: the live entries of each list come first, are distinct, and name fields owned by the block's own sky tile or by the tiles one index below or above it, cyclically over 64 tiles; the remaining entries equal 4096. A list holds 16 or more live entries, and every tile has a block with all 32 live. `owner`: each sky tile owns exactly 64 fields. `slots`: each observation names a live entry of its block's list.
All inputs are finite; a program needn't handle non-finite values.
Results may differ from a plain program's by a relative error of at most 0.00023.
Values sent between devices are 32-bit elements; how exact they have to be, the bound alone decides.
A program may use at most 64 MiB of HBM per device.

v0:
```python
import jax
import jax.numpy as jnp
from jax import lax
from jax.sharding import PartitionSpec as P

COLORS = 8
SWEEPS = 4


PRIOR_WEIGHT = 1.0


def side_by_side(arrays, axis, dim, along):
    ends, at = ([], 0)
    for a in arrays[:-1]:
        at += a.shape[along]
        ends.append(at)
    both = jnp.concatenate(arrays, axis=along)
    return tuple(jnp.split(lax.all_gather(both, axis, axis=dim, tiled=True), ends, axis=along))


def from_behind(value, axis, steps):
    count = lax.axis_size(axis)
    pairs = [(source, (source + steps) % count) for source in range(count)]
    return lax.ppermute(value, axis, pairs)


def from_everyone(shard, axis):
    size = lax.axis_size(axis)
    return lax.all_to_all(
        jnp.broadcast_to(shard[None], (size, *shard.shape)), axis, 0, 0, tiled=True
    )


def over_copies(shard, axis):
    everything = from_everyone(shard, axis)
    return jnp.sum(everything, axis=0)


def body(magnitudes, weights, slots, block_fields, owner, colors, color_terms):
    band_count = color_terms.shape[0]
    tiles = lax.axis_size("sky")
    my_tile = lax.axis_index("sky")
    my_band = lax.axis_index("band")
    band_mags, band_wts = side_by_side((magnitudes, weights), "band", 0, 1)
    band_slots = lax.all_gather(slots, "band", axis=0, tiled=True)
    band_rows, obs_count, star_count = band_mags.shape
    block_count, list_len = block_fields.shape
    block_rows = star_count // block_count
    fields = owner.shape[0]
    slot_grid = band_slots.reshape(band_rows, obs_count, block_count, block_rows)
    entries = jnp.arange(list_len, dtype=jnp.int32)
    star_weight = jnp.sum(band_wts, axis=1)
    mixing = (
        jnp.eye(band_count, dtype=jnp.float32)
        + color_terms
        - jnp.diag(jnp.sum(color_terms, axis=1))
    )
    owner_order = jnp.argsort(owner, stable=True)
    owned = fields // tiles

    def slot_sums(values):
        grid = values.reshape(band_rows, obs_count, block_count, block_rows)
        hits = slot_grid[..., None] == entries
        return jnp.sum(jnp.where(hits, grid[..., None], 0.0), axis=(1, 3))

    def spread(list_vals):
        hits = slot_grid[..., None] == entries
        picked = jnp.sum(jnp.where(hits, list_vals[:, None, :, None, :], 0.0), axis=4)
        return picked.reshape(band_rows, obs_count, star_count)

    def predict(zp_obs):
        star_means = jnp.sum(band_wts * (band_mags - zp_obs), axis=1) / star_weight
        predicted = jnp.dot(mixing, star_means, precision=lax.Precision.HIGHEST)
        return (star_means, predicted)

    positions = jnp.argsort(owner_order, stable=True)
    rank_in = positions - owner * owned
    live = block_fields < fields
    safe_ids = jnp.minimum(block_fields, fields - 1)
    relative = jnp.mod(jnp.take(owner, safe_ids) - my_tile + 1, tiles)
    list_ids = jnp.where(live, relative * owned + jnp.take(rank_in, safe_ids), 3 * owned)
    segments = 3 * owned
    nearby_idx = jnp.mod(my_tile + jnp.arange(3, dtype=jnp.int32) - 1, tiles)
    near_fields = jnp.take(owner_order.reshape(tiles, owned), nearby_idx, axis=0)
    zp_colors = jnp.take(colors, near_fields)[None]
    zero_pts = jnp.zeros((band_rows, 3, owned), jnp.float32)

    def flatten(table):
        return table.reshape(band_rows, 3 * owned)

    def combine(partial_flat):
        partial_sums = partial_flat.reshape(band_rows, 3, owned)
        from_left = from_behind(partial_sums[:, 1:3], "sky", 1)
        from_right = from_behind(partial_sums[:, 0:2], "sky", -1)
        far_left = from_behind(partial_sums[:, 2], "sky", 2)
        far_right = from_behind(partial_sums[:, 0], "sky", -2)
        below = far_left + from_left[:, 0] + partial_sums[:, 0]
        middle = from_left[:, 1] + partial_sums[:, 1] + from_right[:, 0]
        above = partial_sums[:, 2] + from_right[:, 1] + far_right
        return jnp.stack([below, middle, above], axis=1)

    def lookup(table):
        padded = jnp.concatenate([flatten(table), jnp.zeros((band_rows, 1), jnp.float32)], axis=1)
        return spread(jnp.take(padded, list_ids, axis=1))

    def segment_band(per_band):
        return jax.ops.segment_sum(
            per_band.reshape(-1), list_ids.reshape(-1), num_segments=segments + 1
        )[:segments]

    def totals(values):
        per_slot = slot_sums(values)
        return combine(jax.vmap(segment_band)(per_slot))

    denominators = totals(band_wts) + PRIOR_WEIGHT

    def squared_misfit(residual, zp_obs):
        per_band = jnp.sum(band_wts * (residual - zp_obs) ** 2, axis=(1, 2))
        return lax.dynamic_index_in_dim(per_band, my_band, 0, keepdims=False)

    def advance(table, color_no):
        zp_obs = lookup(table)
        star_means, predicted = predict(zp_obs)
        residual = band_mags - predicted[:, None, :]
        updated = totals(band_wts * residual) / denominators
        local_value = squared_misfit(residual, zp_obs)
        return (jnp.where(zp_colors == color_no, updated, table), local_value)

    def later_colors(color_no, table):
        return advance(table, color_no)[0]

    recorded = []
    for sweep_no in range(SWEEPS):
        zero_pts, local_value = advance(zero_pts, 0)
        if sweep_no > 0:
            recorded.append(local_value)
        zero_pts = lax.fori_loop(1, COLORS, later_colors, zero_pts)
    zp_obs = lookup(zero_pts)
    star_means, predicted = predict(zp_obs)
    residual = band_mags - predicted[:, None, :]
    recorded.append(squared_misfit(residual, zp_obs))
    stacked = jnp.stack(recorded)
    stacked = over_copies(stacked, "sky")
    misfit = stacked / (obs_count * star_count * tiles)
    own_zp = lax.dynamic_index_in_dim(zero_pts[:, 1], my_band, 0, keepdims=True)
    own_means = lax.dynamic_index_in_dim(star_means, my_band, 0, keepdims=True)
    return (own_zp, own_means, misfit[:, None])


def solution(mesh):
    in_specs = (
        P("band", None, "sky"),
        P("band", None, "sky"),
        P("band", None, "sky"),
        P("sky", None),
        P(),
        P(),
        P(),
    )
    out_specs = (P("band", "sky"), P("band", "sky"), P(None, "band"))
    return jax.shard_map(body, mesh=mesh, in_specs=in_specs, out_specs=out_specs, check_vma=False)
```

profile of v0, /device:TPU:2, one launch (start us, length us, event | category | flops | bytes accessed | tf_op | source)
XLA Modules:
  0.0 707.8 jit_solution(7759130356190868759)
XLA Ops:
  71.9 136.4 %while.60 = (s32[]{:T(128)}, f32[4,3,64]{2,0,1:T(4,128)S(1)}, s32[1,3,64]{2,1,0:T(4,128)S(1)}, s32[8,32]{1,0:T(8,128)S(1)}, s32[4,8,2048]{2,1,0:T(8,128)S(1)}, /...) while((s32[]{:T(128)}, f32[4,3,64]{2,0,1:T(4,128)S(1)}, ...), condition=%wide.wide.region_15.18_spmd.clone, body=%wide.wide.region_10.17_spmd.clone.sunk | while | flops 13247426 | bytes 4053001 | solution.py:138
  78.7 8.7 %collective-permute-start = (f32[4,64]{1,0:T(4,128)S(1)}, f32[4,64]{1,0:T(4,128)S(1)}, u32[]{:S(2)}, u32[]{:S(2)}) collective-permute-start(f32[4,64]{1,0:T(4,128)S(1)} %bitcast.683), channel_id=1, source_target_pairs={{0,248},{4,252},{8,0},{12,4},{16,8},{20,12},{24,16},{28,20},{32,24... | collective-permute-start | bytes 3080 | tf_op jit(solution)/shard_map/while/body/eval_jaxpr/ppermute | solution.py:25
  98.5 8.6 %collective-permute-start = (f32[4,64]{1,0:T(4,128)S(1)}, f32[4,64]{1,0:T(4,128)S(1)}, u32[]{:S(2)}, u32[]{:S(2)}) collective-permute-start(f32[4,64]{1,0:T(4,128)S(1)} %bitcast.683), channel_id=1, source_target_pairs={{0,248},{4,252},{8,0},{12,4},{16,8},{20,12},{24,16},{28,20},{32,24... | collective-permute-start | bytes 3080 | tf_op jit(solution)/shard_map/while/body/eval_jaxpr/ppermute | solution.py:25
  117.8 8.6 %collective-permute-start = (f32[4,64]{1,0:T(4,128)S(1)}, f32[4,64]{1,0:T(4,128)S(1)}, u32[]{:S(2)}, u32[]{:S(2)}) collective-permute-start(f32[4,64]{1,0:T(4,128)S(1)} %bitcast.683), channel_id=1, source_target_pairs={{0,248},{4,252},{8,0},{12,4},{16,8},{20,12},{24,16},{28,20},{32,24... | collective-permute-start | bytes 3080 | tf_op jit(solution)/shard_map/while/body/eval_jaxpr/ppermute | solution.py:25
  137.6 8.6 %collective-permute-start = (f32[4,64]{1,0:T(4,128)S(1)}, f32[4,64]{1,0:T(4,128)S(1)}, u32[]{:S(2)}, u32[]{:S(2)}) collective-permute-start(f32[4,64]{1,0:T(4,128)S(1)} %bitcast.683), channel_id=1, source_target_pairs={{0,248},{4,252},{8,0},{12,4},{16,8},{20,12},{24,16},{28,20},{32,24... | collective-permute-start | bytes 3080 | tf_op jit(solution)/shard_map/while/body/eval_jaxpr/ppermute | solution.py:25
  156.8 8.6 %collective-permute-start = (f32[4,64]{1,0:T(4,128)S(1)}, f32[4,64]{1,0:T(4,128)S(1)}, u32[]{:S(2)}, u32[]{:S(2)}) collective-permute-start(f32[4,64]{1,0:T(4,128)S(1)} %bitcast.683), channel_id=1, source_target_pairs={{0,248},{4,252},{8,0},{12,4},{16,8},{20,12},{24,16},{28,20},{32,24... | collective-permute-start | bytes 3080 | tf_op jit(solution)/shard_map/while/body/eval_jaxpr/ppermute | solution.py:25
  176.6 8.6 %collective-permute-start = (f32[4,64]{1,0:T(4,128)S(1)}, f32[4,64]{1,0:T(4,128)S(1)}, u32[]{:S(2)}, u32[]{:S(2)}) collective-permute-start(f32[4,64]{1,0:T(4,128)S(1)} %bitcast.683), channel_id=1, source_target_pairs={{0,248},{4,252},{8,0},{12,4},{16,8},{20,12},{24,16},{28,20},{32,24... | collective-permute-start | bytes 3080 | tf_op jit(solution)/shard_map/while/body/eval_jaxpr/ppermute | solution.py:25
  195.9 8.6 %collective-permute-start = (f32[4,64]{1,0:T(4,128)S(1)}, f32[4,64]{1,0:T(4,128)S(1)}, u32[]{:S(2)}, u32[]{:S(2)}) collective-permute-start(f32[4,64]{1,0:T(4,128)S(1)} %bitcast.683), channel_id=1, source_target_pairs={{0,248},{4,252},{8,0},{12,4},{16,8},{20,12},{24,16},{28,20},{32,24... | collective-permute-start | bytes 3080 | tf_op jit(solution)/shard_map/while/body/eval_jaxpr/ppermute | solution.py:25
  227.5 136.7 %while.61 = (s32[]{:T(128)}, f32[4,3,64]{2,0,1:T(4,128)S(1)}, s32[1,3,64]{2,1,0:T(4,128)S(1)}, s32[8,32]{1,0:T(8,128)S(1)}, s32[4,8,2048]{2,1,0:T(8,128)S(1)}, /...) while((s32[]{:T(128)}, f32[4,3,64]{2,0,1:T(4,128)S(1)}, ...), condition=%wide.wide.region_25.28_spmd.clone, body=%wide.wide.region_20.27_spmd.clone.sunk | while | flops 13247426 | bytes 4577289 | solution.py:138
  234.7 8.9 %collective-permute-start.4 = (f32[4,64]{1,0:T(4,128)S(1)}, f32[4,64]{1,0:T(4,128)S(1)}, u32[]{:S(2)}, u32[]{:S(2)}) collective-permute-start(f32[4,64]{1,0:T(4,128)S(1)} %bitcast.684), channel_id=1, source_target_pairs={{0,248},{4,252},{8,0},{12,4},{16,8},{20,12},{24,16},{28,20},{32,24... | collective-permute-start | bytes 3080 | tf_op jit(solution)/shard_map/while/body/eval_jaxpr/ppermute | solution.py:25
  254.2 8.6 %collective-permute-start.4 = (f32[4,64]{1,0:T(4,128)S(1)}, f32[4,64]{1,0:T(4,128)S(1)}, u32[]{:S(2)}, u32[]{:S(2)}) collective-permute-start(f32[4,64]{1,0:T(4,128)S(1)} %bitcast.684), channel_id=1, source_target_pairs={{0,248},{4,252},{8,0},{12,4},{16,8},{20,12},{24,16},{28,20},{32,24... | collective-permute-start | bytes 3080 | tf_op jit(solution)/shard_map/while/body/eval_jaxpr/ppermute | solution.py:25
  273.9 8.6 %collective-permute-start.4 = (f32[4,64]{1,0:T(4,128)S(1)}, f32[4,64]{1,0:T(4,128)S(1)}, u32[]{:S(2)}, u32[]{:S(2)}) collective-permute-start(f32[4,64]{1,0:T(4,128)S(1)} %bitcast.684), channel_id=1, source_target_pairs={{0,248},{4,252},{8,0},{12,4},{16,8},{20,12},{24,16},{28,20},{32,24... | collective-permute-start | bytes 3080 | tf_op jit(solution)/shard_map/while/body/eval_jaxpr/ppermute | solution.py:25
  312.9 8.6 %collective-permute-start.4 = (f32[4,64]{1,0:T(4,128)S(1)}, f32[4,64]{1,0:T(4,128)S(1)}, u32[]{:S(2)}, u32[]{:S(2)}) collective-permute-start(f32[4,64]{1,0:T(4,128)S(1)} %bitcast.684), channel_id=1, source_target_pairs={{0,248},{4,252},{8,0},{12,4},{16,8},{20,12},{24,16},{28,20},{32,24... | collective-permute-start | bytes 3080 | tf_op jit(solution)/shard_map/while/body/eval_jaxpr/ppermute | solution.py:25
  332.2 8.6 %collective-permute-start.4 = (f32[4,64]{1,0:T(4,128)S(1)}, f32[4,64]{1,0:T(4,128)S(1)}, u32[]{:S(2)}, u32[]{:S(2)}) collective-permute-start(f32[4,64]{1,0:T(4,128)S(1)} %bitcast.684), channel_id=1, source_target_pairs={{0,248},{4,252},{8,0},{12,4},{16,8},{20,12},{24,16},{28,20},{32,24... | collective-permute-start | bytes 3080 | tf_op jit(solution)/shard_map/while/body/eval_jaxpr/ppermute | solution.py:25
  351.9 8.6 %collective-permute-start.4 = (f32[4,64]{1,0:T(4,128)S(1)}, f32[4,64]{1,0:T(4,128)S(1)}, u32[]{:S(2)}, u32[]{:S(2)}) collective-permute-start(f32[4,64]{1,0:T(4,128)S(1)} %bitcast.684), channel_id=1, source_target_pairs={{0,248},{4,252},{8,0},{12,4},{16,8},{20,12},{24,16},{28,20},{32,24... | collective-permute-start | bytes 3080 | tf_op jit(solution)/shard_map/while/body/eval_jaxpr/ppermute | solution.py:25
  383.9 136.3 %while.62 = (s32[]{:T(128)}, f32[4,3,64]{2,0,1:T(4,128)S(1)}, s32[1,3,64]{2,1,0:T(4,128)S(1)}, s32[8,32]{1,0:T(8,128)S(1)}, s32[4,8,2048]{2,1,0:T(8,128)S(1)}, /...) while((s32[]{:T(128)}, f32[4,3,64]{2,0,1:T(4,128)S(1)}, ...), condition=%wide.wide.region_35.38_spmd.clone, body=%wide.wide.region_30.37_spmd.clone.sunk | while | flops 13247426 | bytes 4577289 | solution.py:138
  390.8 8.7 %collective-permute-start.8 = (f32[4,64]{1,0:T(4,128)S(1)}, f32[4,64]{1,0:T(4,128)S(1)}, u32[]{:S(2)}, u32[]{:S(2)}) collective-permute-start(f32[4,64]{1,0:T(4,128)S(1)} %bitcast.685), channel_id=1, source_target_pairs={{0,248},{4,252},{8,0},{12,4},{16,8},{20,12},{24,16},{28,20},{32,24... | collective-permute-start | bytes 3080 | tf_op jit(solution)/shard_map/while/body/eval_jaxpr/ppermute | solution.py:25
  410.6 8.6 %collective-permute-start.8 = (f32[4,64]{1,0:T(4,128)S(1)}, f32[4,64]{1,0:T(4,128)S(1)}, u32[]{:S(2)}, u32[]{:S(2)}) collective-permute-start(f32[4,64]{1,0:T(4,128)S(1)} %bitcast.685), channel_id=1, source_target_pairs={{0,248},{4,252},{8,0},{12,4},{16,8},{20,12},{24,16},{28,20},{32,24... | collective-permute-start | bytes 3080 | tf_op jit(solution)/shard_map/while/body/eval_jaxpr/ppermute | solution.py:25
  429.8 8.6 %collective-permute-start.8 = (f32[4,64]{1,0:T(4,128)S(1)}, f32[4,64]{1,0:T(4,128)S(1)}, u32[]{:S(2)}, u32[]{:S(2)}) collective-permute-start(f32[4,64]{1,0:T(4,128)S(1)} %bitcast.685), channel_id=1, source_target_pairs={{0,248},{4,252},{8,0},{12,4},{16,8},{20,12},{24,16},{28,20},{32,24... | collective-permute-start | bytes 3080 | tf_op jit(solution)/shard_map/while/body/eval_jaxpr/ppermute | solution.py:25
  449.6 8.6 %collective-permute-start.8 = (f32[4,64]{1,0:T(4,128)S(1)}, f32[4,64]{1,0:T(4,128)S(1)}, u32[]{:S(2)}, u32[]{:S(2)}) collective-permute-start(f32[4,64]{1,0:T(4,128)S(1)} %bitcast.685), channel_id=1, source_target_pairs={{0,248},{4,252},{8,0},{12,4},{16,8},{20,12},{24,16},{28,20},{32,24... | collective-permute-start | bytes 3080 | tf_op jit(solution)/shard_map/while/body/eval_jaxpr/ppermute | solution.py:25
  468.8 8.6 %collective-permute-start.8 = (f32[4,64]{1,0:T(4,128)S(1)}, f32[4,64]{1,0:T(4,128)S(1)}, u32[]{:S(2)}, u32[]{:S(2)}) collective-permute-start(f32[4,64]{1,0:T(4,128)S(1)} %bitcast.685), channel_id=1, source_target_pairs={{0,248},{4,252},{8,0},{12,4},{16,8},{20,12},{24,16},{28,20},{32,24... | collective-permute-start | bytes 3080 | tf_op jit(solution)/shard_map/while/body/eval_jaxpr/ppermute | solution.py:25
  488.6 8.6 %collective-permute-start.8 = (f32[4,64]{1,0:T(4,128)S(1)}, f32[4,64]{1,0:T(4,128)S(1)}, u32[]{:S(2)}, u32[]{:S(2)}) collective-permute-start(f32[4,64]{1,0:T(4,128)S(1)} %bitcast.685), channel_id=1, source_target_pairs={{0,248},{4,252},{8,0},{12,4},{16,8},{20,12},{24,16},{28,20},{32,24... | collective-permute-start | bytes 3080 | tf_op jit(solution)/shard_map/while/body/eval_jaxpr/ppermute | solution.py:25
  540.1 136.7 %while.63 = (s32[]{:T(128)}, f32[4,3,64]{2,0,1:T(4,128)S(1)}, s32[1,3,64]{2,1,0:T(4,128)S(1)}, s32[8,32]{1,0:T(8,128)S(1)}, s32[4,8,2048]{2,1,0:T(8,128)S(1)}, /...) while((s32[]{:T(128)}, f32[4,3,64]{2,0,1:T(4,128)S(1)}, ...), condition=%wide.wide.region_45.48_spmd.clone, body=%wide.wide.region_40.47_spmd.clone.sunk | while | flops 13247426 | bytes 4577289 | solution.py:138
  547.2 8.8 %collective-permute-start.12 = (f32[4,64]{1,0:T(4,128)S(1)}, f32[4,64]{1,0:T(4,128)S(1)}, u32[]{:S(2)}, u32[]{:S(2)}) collective-permute-start(f32[4,64]{1,0:T(4,128)S(1)} %bitcast.686), channel_id=1, source_target_pairs={{0,248},{4,252},{8,0},{12,4},{16,8},{20,12},{24,16},{28,20},{32,24... | collective-permute-start | bytes 3080 | tf_op jit(solution)/shard_map/while/body/eval_jaxpr/ppermute | solution.py:25
  566.7 8.6 %collective-permute-start.12 = (f32[4,64]{1,0:T(4,128)S(1)}, f32[4,64]{1,0:T(4,128)S(1)}, u32[]{:S(2)}, u32[]{:S(2)}) collective-permute-start(f32[4,64]{1,0:T(4,128)S(1)} %bitcast.686), channel_id=1, source_target_pairs={{0,248},{4,252},{8,0},{12,4},{16,8},{20,12},{24,16},{28,20},{32,24... | collective-permute-start | bytes 3080 | tf_op jit(solution)/shard_map/while/body/eval_jaxpr/ppermute | solution.py:25
  586.4 8.6 %collective-permute-start.12 = (f32[4,64]{1,0:T(4,128)S(1)}, f32[4,64]{1,0:T(4,128)S(1)}, u32[]{:S(2)}, u32[]{:S(2)}) collective-permute-start(f32[4,64]{1,0:T(4,128)S(1)} %bitcast.686), channel_id=1, source_target_pairs={{0,248},{4,252},{8,0},{12,4},{16,8},{20,12},{24,16},{28,20},{32,24... | collective-permute-start | bytes 3080 | tf_op jit(solution)/shard_map/while/body/eval_jaxpr/ppermute | solution.py:25
  605.7 8.6 %collective-permute-start.12 = (f32[4,64]{1,0:T(4,128)S(1)}, f32[4,64]{1,0:T(4,128)S(1)}, u32[]{:S(2)}, u32[]{:S(2)}) collective-permute-start(f32[4,64]{1,0:T(4,128)S(1)} %bitcast.686), channel_id=1, source_target_pairs={{0,248},{4,252},{8,0},{12,4},{16,8},{20,12},{24,16},{28,20},{32,24... | collective-permute-start | bytes 3080 | tf_op jit(solution)/shard_map/while/body/eval_jaxpr/ppermute | solution.py:25
  625.4 8.6 %collective-permute-start.12 = (f32[4,64]{1,0:T(4,128)S(1)}, f32[4,64]{1,0:T(4,128)S(1)}, u32[]{:S(2)}, u32[]{:S(2)}) collective-permute-start(f32[4,64]{1,0:T(4,128)S(1)} %bitcast.686), channel_id=1, source_target_pairs={{0,248},{4,252},{8,0},{12,4},{16,8},{20,12},{24,16},{28,20},{32,24... | collective-permute-start | bytes 3080 | tf_op jit(solution)/shard_map/while/body/eval_jaxpr/ppermute | solution.py:25
  644.7 8.6 %collective-permute-start.12 = (f32[4,64]{1,0:T(4,128)S(1)}, f32[4,64]{1,0:T(4,128)S(1)}, u32[]{:S(2)}, u32[]{:S(2)}) collective-permute-start(f32[4,64]{1,0:T(4,128)S(1)} %bitcast.686), channel_id=1, source_target_pairs={{0,248},{4,252},{8,0},{12,4},{16,8},{20,12},{24,16},{28,20},{32,24... | collective-permute-start | bytes 3080 | tf_op jit(solution)/shard_map/while/body/eval_jaxpr/ppermute | solution.py:25
  664.4 8.6 %collective-permute-start.12 = (f32[4,64]{1,0:T(4,128)S(1)}, f32[4,64]{1,0:T(4,128)S(1)}, u32[]{:S(2)}, u32[]{:S(2)}) collective-permute-start(f32[4,64]{1,0:T(4,128)S(1)} %bitcast.686), channel_id=1, source_target_pairs={{0,248},{4,252},{8,0},{12,4},{16,8},{20,12},{24,16},{28,20},{32,24... | collective-permute-start | bytes 3080 | tf_op jit(solution)/shard_map/while/body/eval_jaxpr/ppermute | solution.py:25
  685.3 9.6 %all-to-all-start = ((f32[64,1,4]{2,1,0:T(1,128)}), f32[64,1,4]{2,1,0:T(1,128)S(1)}, u32[]{:S(2)}, u32[]{:S(2)}) async-start(f32[64,1,4]{2,1,0:T(1,128)} %broadcast_in_dim.458), calls=%async_computation | async-start | bytes 65536 | tf_op jit(solution)/shard_map/all_to_all | solution.py:30
  695.5 11.5 %all-to-all-done = f32[64,1,4]{2,1,0:T(1,128)S(1)} async-done(((f32[64,1,4]{2,1,0:T(1,128)}), f32[64,1,4]{2,1,0:T(1,128)S(1)}, u32[]{:S(2)}, u32[]{:S(2)}) %all-to-all-start) | async-done | bytes 1056 | tf_op jit(solution)/shard_map/all_to_all | solution.py:30
  (1348 shorter events, 455.4 us)
Async XLA Ops:
  40.6 18.6 %collective-permute-start.16 = (f32[4,64]{1,0:T(4,128)S(1)}, f32[4,64]{1,0:T(4,128)S(1)}, u32[]{:S(2)}, u32[]{:S(2)}) collective-permute-start(f32[4,64]{1,0:T(4,128)S(1)} %bitcast.697), channel_id=1, source_target_pairs={{0,8},{4,12},{8,16},{12,20},{16,24},{20,28},{24,32},{28,36},{32,40... | collective-permute-start | bytes 3080 | tf_op jit(solution)/shard_map/ppermute | solution.py:25
  43.2 16.0 %collective-permute-start.17 = (f32[4,2,64]{2,0,1:T(4,128)S(1)}, f32[4,2,64]{2,0,1:T(4,128)S(1)}, u32[]{:S(2)}, u32[]{:S(2)}) collective-permute-start(f32[4,2,64]{2,0,1:T(4,128)S(1)} %copy.336), channel_id=1, source_target_pairs={{0,4},{4,8},{8,12},{12,16},{16,20},{20,24},{24,28},{28,32},{32,36}... | collective-permute-start | bytes 6152 | tf_op jit(solution)/shard_map/ppermute | solution.py:25
  45.2 21.7 %collective-permute-start.18 = (f32[4,2,64]{2,0,1:T(4,128)S(1)}, f32[4,2,64]{2,0,1:T(4,128)S(1)}, u32[]{:S(2)}, u32[]{:S(2)}) collective-permute-start(f32[4,2,64]{2,0,1:T(4,128)S(1)} %copy.339), channel_id=1, source_target_pairs={{0,252},{4,0},{8,4},{12,8},{16,12},{20,16},{24,20},{28,24},{32,28}... | collective-permute-start | bytes 6152 | tf_op jit(solution)/shard_map/ppermute | solution.py:25
  51.4 17.8 %collective-permute-start.19 = (f32[4,64]{1,0:T(4,128)S(1)}, f32[4,64]{1,0:T(4,128)S(1)}, u32[]{:S(2)}, u32[]{:S(2)}) collective-permute-start(f32[4,64]{1,0:T(4,128)S(1)} %bitcast.698), channel_id=1, source_target_pairs={{0,248},{4,252},{8,0},{12,4},{16,8},{20,12},{24,16},{28,20},{32,24... | collective-permute-start | bytes 3080 | tf_op jit(solution)/shard_map/ppermute | solution.py:25
  58.1 11.1 %collective-permute-start.20 = (f32[4,64]{1,0:T(4,128)S(1)}, f32[4,64]{1,0:T(4,128)S(1)}, u32[]{:S(2)}, u32[]{:S(2)}) collective-permute-start(f32[4,64]{1,0:T(4,128)S(1)} %bitcast.699), channel_id=1, source_target_pairs={{0,8},{4,12},{8,16},{12,20},{16,24},{20,28},{24,32},{28,36},{32,40... | collective-permute-start | bytes 3080 | tf_op jit(solution)/shard_map/ppermute | solution.py:25
  78.5 11.1 %collective-permute-start.3 = (f32[4,64]{1,0:T(4,128)S(1)}, f32[4,64]{1,0:T(4,128)S(1)}, u32[]{:S(2)}, u32[]{:S(2)}) collective-permute-start(f32[4,64]{1,0:T(4,128)S(1)} %bitcast.679), channel_id=1, source_target_pairs={{0,8},{4,12},{8,16},{12,20},{16,24},{20,28},{24,32},{28,36},{32,40... | collective-permute-start | bytes 3080 | tf_op jit(solution)/shard_map/while/body/eval_jaxpr/ppermute | solution.py:25
  97.7 11.1 %collective-permute-start.3 = (f32[4,64]{1,0:T(4,128)S(1)}, f32[4,64]{1,0:T(4,128)S(1)}, u32[]{:S(2)}, u32[]{:S(2)}) collective-permute-start(f32[4,64]{1,0:T(4,128)S(1)} %bitcast.679), channel_id=1, source_target_pairs={{0,8},{4,12},{8,16},{12,20},{16,24},{20,28},{24,32},{28,36},{32,40... | collective-permute-start | bytes 3080 | tf_op jit(solution)/shard_map/while/body/eval_jaxpr/ppermute | solution.py:25
  117.5 11.1 %collective-permute-start.3 = (f32[4,64]{1,0:T(4,128)S(1)}, f32[4,64]{1,0:T(4,128)S(1)}, u32[]{:S(2)}, u32[]{:S(2)}) collective-permute-start(f32[4,64]{1,0:T(4,128)S(1)} %bitcast.679), channel_id=1, source_target_pairs={{0,8},{4,12},{8,16},{12,20},{16,24},{20,28},{24,32},{28,36},{32,40... | collective-permute-start | bytes 3080 | tf_op jit(solution)/shard_map/while/body/eval_jaxpr/ppermute | solution.py:25
  136.8 11.1 %collective-permute-start.3 = (f32[4,64]{1,0:T(4,128)S(1)}, f32[4,64]{1,0:T(4,128)S(1)}, u32[]{:S(2)}, u32[]{:S(2)}) collective-permute-start(f32[4,64]{1,0:T(4,128)S(1)} %bitcast.679), channel_id=1, source_target_pairs={{0,8},{4,12},{8,16},{12,20},{16,24},{20,28},{24,32},{28,36},{32,40... | collective-permute-start | bytes 3080 | tf_op jit(solution)/shard_map/while/body/eval_jaxpr/ppermute | solution.py:25
  156.6 11.1 %collective-permute-start.3 = (f32[4,64]{1,0:T(4,128)S(1)}, f32[4,64]{1,0:T(4,128)S(1)}, u32[]{:S(2)}, u32[]{:S(2)}) collective-permute-start(f32[4,64]{1,0:T(4,128)S(1)} %bitcast.679), channel_id=1, source_target_pairs={{0,8},{4,12},{8,16},{12,20},{16,24},{20,28},{24,32},{28,36},{32,40... | collective-permute-start | bytes 3080 | tf_op jit(solution)/shard_map/while/body/eval_jaxpr/ppermute | solution.py:25
  175.8 11.1 %collective-permute-start.3 = (f32[4,64]{1,0:T(4,128)S(1)}, f32[4,64]{1,0:T(4,128)S(1)}, u32[]{:S(2)}, u32[]{:S(2)}) collective-permute-start(f32[4,64]{1,0:T(4,128)S(1)} %bitcast.679), channel_id=1, source_target_pairs={{0,8},{4,12},{8,16},{12,20},{16,24},{20,28},{24,32},{28,36},{32,40... | collective-permute-start | bytes 3080 | tf_op jit(solution)/shard_map/while/body/eval_jaxpr/ppermute | solution.py:25
  195.6 11.1 %collective-permute-start.3 = (f32[4,64]{1,0:T(4,128)S(1)}, f32[4,64]{1,0:T(4,128)S(1)}, u32[]{:S(2)}, u32[]{:S(2)}) collective-permute-start(f32[4,64]{1,0:T(4,128)S(1)} %bitcast.679), channel_id=1, source_target_pairs={{0,8},{4,12},{8,16},{12,20},{16,24},{20,28},{24,32},{28,36},{32,40... | collective-permute-start | bytes 3080 | tf_op jit(solution)/shard_map/while/body/eval_jaxpr/ppermute | solution.py:25
  214.8 11.1 %collective-permute-start.25 = (f32[4,2,64]{2,0,1:T(4,128)S(1)}, f32[4,2,64]{2,0,1:T(4,128)S(1)}, u32[]{:S(2)}, u32[]{:S(2)}) collective-permute-start(f32[4,2,64]{2,0,1:T(4,128)S(1)} %copy.346), channel_id=1, source_target_pairs={{0,4},{4,8},{8,12},{12,16},{16,20},{20,24},{24,28},{28,32},{32,36}... | collective-permute-start | bytes 6152 | tf_op jit(solution)/shard_map/ppermute | solution.py:25
  234.1 11.1 %collective-permute-start.7 = (f32[4,64]{1,0:T(4,128)S(1)}, f32[4,64]{1,0:T(4,128)S(1)}, u32[]{:S(2)}, u32[]{:S(2)}) collective-permute-start(f32[4,64]{1,0:T(4,128)S(1)} %bitcast.680), channel_id=1, source_target_pairs={{0,8},{4,12},{8,16},{12,20},{16,24},{20,28},{24,32},{28,36},{32,40... | collective-permute-start | bytes 3080 | tf_op jit(solution)/shard_map/while/body/eval_jaxpr/ppermute | solution.py:25
  253.8 11.1 %collective-permute-start.7 = (f32[4,64]{1,0:T(4,128)S(1)}, f32[4,64]{1,0:T(4,128)S(1)}, u32[]{:S(2)}, u32[]{:S(2)}) collective-permute-start(f32[4,64]{1,0:T(4,128)S(1)} %bitcast.680), channel_id=1, source_target_pairs={{0,8},{4,12},{8,16},{12,20},{16,24},{20,28},{24,32},{28,36},{32,40... | collective-permute-start | bytes 3080 | tf_op jit(solution)/shard_map/while/body/eval_jaxpr/ppermute | solution.py:25
  292.9 11.1 %collective-permute-start.7 = (f32[4,64]{1,0:T(4,128)S(1)}, f32[4,64]{1,0:T(4,128)S(1)}, u32[]{:S(2)}, u32[]{:S(2)}) collective-permute-start(f32[4,64]{1,0:T(4,128)S(1)} %bitcast.680), channel_id=1, source_target_pairs={{0,8},{4,12},{8,16},{12,20},{16,24},{20,28},{24,32},{28,36},{32,40... | collective-permute-start | bytes 3080 | tf_op jit(solution)/shard_map/while/body/eval_jaxpr/ppermute | solution.py:25
  331.9 11.1 %collective-permute-start.7 = (f32[4,64]{1,0:T(4,128)S(1)}, f32[4,64]{1,0:T(4,128)S(1)}, u32[]{:S(2)}, u32[]{:S(2)}) collective-permute-start(f32[4,64]{1,0:T(4,128)S(1)} %bitcast.680), channel_id=1, source_target_pairs={{0,8},{4,12},{8,16},{12,20},{16,24},{20,28},{24,32},{28,36},{32,40... | collective-permute-start | bytes 3080 | tf_op jit(solution)/shard_map/while/body/eval_jaxpr/ppermute | solution.py:25
  351.1 11.1 %collective-permute-start.7 = (f32[4,64]{1,0:T(4,128)S(1)}, f32[4,64]{1,0:T(4,128)S(1)}, u32[]{:S(2)}, u32[]{:S(2)}) collective-permute-start(f32[4,64]{1,0:T(4,128)S(1)} %bitcast.680), channel_id=1, source_target_pairs={{0,8},{4,12},{8,16},{12,20},{16,24},{20,28},{24,32},{28,36},{32,40... | collective-permute-start | bytes 3080 | tf_op jit(solution)/shard_map/while/body/eval_jaxpr/ppermute | solution.py:25
  371.1 11.2 %collective-permute-start.29 = (f32[4,2,64]{2,0,1:T(4,128)S(1)}, f32[4,2,64]{2,0,1:T(4,128)S(1)}, u32[]{:S(2)}, u32[]{:S(2)}) collective-permute-start(f32[4,2,64]{2,0,1:T(4,128)S(1)} %copy.351), channel_id=1, source_target_pairs={{0,4},{4,8},{8,12},{12,16},{16,20},{20,24},{24,28},{28,32},{32,36}... | collective-permute-start | bytes 6152 | tf_op jit(solution)/shard_map/ppermute | solution.py:25
  390.5 11.1 %collective-permute-start.11 = (f32[4,64]{1,0:T(4,128)S(1)}, f32[4,64]{1,0:T(4,128)S(1)}, u32[]{:S(2)}, u32[]{:S(2)}) collective-permute-start(f32[4,64]{1,0:T(4,128)S(1)} %bitcast.681), channel_id=1, source_target_pairs={{0,8},{4,12},{8,16},{12,20},{16,24},{20,28},{24,32},{28,36},{32,40... | collective-permute-start | bytes 3080 | tf_op jit(solution)/shard_map/while/body/eval_jaxpr/ppermute | solution.py:25
  409.8 11.1 %collective-permute-start.11 = (f32[4,64]{1,0:T(4,128)S(1)}, f32[4,64]{1,0:T(4,128)S(1)}, u32[]{:S(2)}, u32[]{:S(2)}) collective-permute-start(f32[4,64]{1,0:T(4,128)S(1)} %bitcast.681), channel_id=1, source_target_pairs={{0,8},{4,12},{8,16},{12,20},{16,24},{20,28},{24,32},{28,36},{32,40... | collective-permute-start | bytes 3080 | tf_op jit(solution)/shard_map/while/body/eval_jaxpr/ppermute | solution.py:25
  429.5 11.1 %collective-permute-start.11 = (f32[4,64]{1,0:T(4,128)S(1)}, f32[4,64]{1,0:T(4,128)S(1)}, u32[]{:S(2)}, u32[]{:S(2)}) collective-permute-start(f32[4,64]{1,0:T(4,128)S(1)} %bitcast.681), channel_id=1, source_target_pairs={{0,8},{4,12},{8,16},{12,20},{16,24},{20,28},{24,32},{28,36},{32,40... | collective-permute-start | bytes 3080 | tf_op jit(solution)/shard_map/while/body/eval_jaxpr/ppermute | solution.py:25
  448.8 11.1 %collective-permute-start.11 = (f32[4,64]{1,0:T(4,128)S(1)}, f32[4,64]{1,0:T(4,128)S(1)}, u32[]{:S(2)}, u32[]{:S(2)}) collective-permute-start(f32[4,64]{1,0:T(4,128)S(1)} %bitcast.681), channel_id=1, source_target_pairs={{0,8},{4,12},{8,16},{12,20},{16,24},{20,28},{24,32},{28,36},{32,40... | collective-permute-start | bytes 3080 | tf_op jit(solution)/shard_map/while/body/eval_jaxpr/ppermute | solution.py:25
  487.8 11.1 %collective-permute-start.11 = (f32[4,64]{1,0:T(4,128)S(1)}, f32[4,64]{1,0:T(4,128)S(1)}, u32[]{:S(2)}, u32[]{:S(2)}) collective-permute-start(f32[4,64]{1,0:T(4,128)S(1)} %bitcast.681), channel_id=1, source_target_pairs={{0,8},{4,12},{8,16},{12,20},{16,24},{20,28},{24,32},{28,36},{32,40... | collective-permute-start | bytes 3080 | tf_op jit(solution)/shard_map/while/body/eval_jaxpr/ppermute | solution.py:25
  507.6 11.1 %collective-permute-start.11 = (f32[4,64]{1,0:T(4,128)S(1)}, f32[4,64]{1,0:T(4,128)S(1)}, u32[]{:S(2)}, u32[]{:S(2)}) collective-permute-start(f32[4,64]{1,0:T(4,128)S(1)} %bitcast.681), channel_id=1, source_target_pairs={{0,8},{4,12},{8,16},{12,20},{16,24},{20,28},{24,32},{28,36},{32,40... | collective-permute-start | bytes 3080 | tf_op jit(solution)/shard_map/while/body/eval_jaxpr/ppermute | solution.py:25
  526.8 12.3 %collective-permute-start.33 = (f32[4,2,64]{2,0,1:T(4,128)S(1)}, f32[4,2,64]{2,0,1:T(4,128)S(1)}, u32[]{:S(2)}, u32[]{:S(2)}) collective-permute-start(f32[4,2,64]{2,0,1:T(4,128)S(1)} %copy.356), channel_id=1, source_target_pairs={{0,4},{4,8},{8,12},{12,16},{16,20},{20,24},{24,28},{28,32},{32,36}... | collective-permute-start | bytes 6152 | tf_op jit(solution)/shard_map/ppermute | solution.py:25
  527.5 11.6 %collective-permute-start.32 = (f32[4,64]{1,0:T(4,128)S(1)}, f32[4,64]{1,0:T(4,128)S(1)}, u32[]{:S(2)}, u32[]{:S(2)}) collective-permute-start(f32[4,64]{1,0:T(4,128)S(1)} %bitcast.701), channel_id=1, source_target_pairs={{0,8},{4,12},{8,16},{12,20},{16,24},{20,28},{24,32},{28,36},{32,40... | collective-permute-start | bytes 3080 | tf_op jit(solution)/shard_map/ppermute | solution.py:25
  546.7 11.1 %collective-permute-start.15 = (f32[4,64]{1,0:T(4,128)S(1)}, f32[4,64]{1,0:T(4,128)S(1)}, u32[]{:S(2)}, u32[]{:S(2)}) collective-permute-start(f32[4,64]{1,0:T(4,128)S(1)} %bitcast.682), channel_id=1, source_target_pairs={{0,8},{4,12},{8,16},{12,20},{16,24},{20,28},{24,32},{28,36},{32,40... | collective-permute-start | bytes 3080 | tf_op jit(solution)/shard_map/while/body/eval_jaxpr/ppermute | solution.py:25
  566.4 11.1 %collective-permute-start.15 = (f32[4,64]{1,0:T(4,128)S(1)}, f32[4,64]{1,0:T(4,128)S(1)}, u32[]{:S(2)}, u32[]{:S(2)}) collective-permute-start(f32[4,64]{1,0:T(4,128)S(1)} %bitcast.682), channel_id=1, source_target_pairs={{0,8},{4,12},{8,16},{12,20},{16,24},{20,28},{24,32},{28,36},{32,40... | collective-permute-start | bytes 3080 | tf_op jit(solution)/shard_map/while/body/eval_jaxpr/ppermute | solution.py:25
  585.7 11.1 %collective-permute-start.15 = (f32[4,64]{1,0:T(4,128)S(1)}, f32[4,64]{1,0:T(4,128)S(1)}, u32[]{:S(2)}, u32[]{:S(2)}) collective-permute-start(f32[4,64]{1,0:T(4,128)S(1)} %bitcast.682), channel_id=1, source_target_pairs={{0,8},{4,12},{8,16},{12,20},{16,24},{20,28},{24,32},{28,36},{32,40... | collective-permute-start | bytes 3080 | tf_op jit(solution)/shard_map/while/body/eval_jaxpr/ppermute | solution.py:25
  605.4 11.1 %collective-permute-start.15 = (f32[4,64]{1,0:T(4,128)S(1)}, f32[4,64]{1,0:T(4,128)S(1)}, u32[]{:S(2)}, u32[]{:S(2)}) collective-permute-start(f32[4,64]{1,0:T(4,128)S(1)} %bitcast.682), channel_id=1, source_target_pairs={{0,8},{4,12},{8,16},{12,20},{16,24},{20,28},{24,32},{28,36},{32,40... | collective-permute-start | bytes 3080 | tf_op jit(solution)/shard_map/while/body/eval_jaxpr/ppermute | solution.py:25
  685.3 21.6 %all-to-all-start = ((f32[64,1,4]{2,1,0:T(1,128)}), f32[64,1,4]{2,1,0:T(1,128)S(1)}, u32[]{:S(2)}, u32[]{:S(2)}) async-start(f32[64,1,4]{2,1,0:T(1,128)} %broadcast_in_dim.458), calls=%async_computation | async-start | bytes 65536 | tf_op jit(solution)/shard_map/all_to_all | solution.py:30
  (108 other events, 945.6 us)
where the time goes:
time: 717 us; the launch traced here: 708 us
  starting transfers between devices  366 us (51%)
  other arithmetic  179 us (25%)
  local copies, waits for them, and re-layouts  68.8 us (10%)
  waiting for transfers between devices  68.1 us (9%)
  blocking collectives  13.8 us (2%)
    ppermute x132, starting transfers between devices, from_behind(): return lax.ppermute(value, axis, pairs)  356 us
    reduce_sum x33, other arithmetic, spread(): jnp.sum(jnp.where(hits, list_vals[:, None, :, None, :], 0.0), axis=4)  60.5 us
    ppermute x132, waiting for transfers between devices, from_behind(): return lax.ppermute(value, axis, pairs)  56.6 us
    scatter-add x33, other arithmetic, segment_band(): jax.ops.segment_sum(per_band.reshape(-1), list_ids.reshape(-1), num_segme...  50.6 us
    reduce_sum x32, other arithmetic, slot_sums(): return jnp.sum(jnp.where(hits, grid[..., None], 0.0), axis=(1, 3))  38.9 us
    gather x33, local copies, waits for them, and re-layouts, lookup(): return spread(jnp.take(padded, list_ids, axis=1))  24.1 us
  transfers between devices with their start and end apart: 133, of which 33 were waited for; matrix products, arithmetic and copies ran while one was open for 2% of the time, Pallas kernels for 0%

commit v1 on v0

v1 whole, which is shorter than its diff:
```python
import functools

import jax
import jax.numpy as jnp
from jax import lax
from jax.experimental import pallas as pl
from jax.experimental.pallas import tpu as pltpu
from jax.sharding import PartitionSpec as P

COLORS = 8
SWEEPS = 4
PRIOR_WEIGHT = 1.0

TILES = 64
BANDS = 4
OBS = 8
BLOCKS = 8
ROWS = 256
STARS = BLOCKS * ROWS
LIST = 32
OWN = 64
NEAR = 3 * OWN
WIDE = BANDS * NEAR
STEPS = COLORS * SWEEPS
MESH = pl.DeviceIdType.MESH
HIGH = lax.Precision.HIGHEST
F32 = jnp.float32
BF16 = jnp.bfloat16
A_MEAN, A_P, A_BF, A_NF, A_COL, A_END = 0, 256, 384, 512, 640, 768


def home_of(tile):
    half = tile // 32
    row = tile // 8
    y = row % 4
    z = tile % 8
    leg = z // 4
    y_new = y + half * (3 - 2 * y)
    z_new = z + leg * (7 - 2 * z)
    x_lo = (1 - half + row + leg) % 2
    return half * 32 + y_new * 8 + z_new, x_lo * 2 + 1


def tile_at(sky, band):
    half = sky // 32
    y_new = (sky // 8) % 4
    z_new = sky % 8
    y = y_new + half * (3 - 2 * y_new)
    row = half * 4 + y
    leg = (band // 2 + 1 + half + row) % 2
    z = z_new + leg * (7 - 2 * z_new)
    is_home = (band % 2 == 1) & (z_new < 4)
    return is_home, (row * 8 + z) % TILES


def iota(shape, dim):
    return lax.broadcasted_iota(jnp.int32, shape, dim)


def as_column(row, count):
    eye = iota((count, 128), 0) == iota((count, 128), 1)
    full = jnp.broadcast_to(row, (count, 128))
    return jnp.sum(jnp.where(eye, full, 0.0), axis=1, keepdims=True)


def ship_kernel(w_ref, s_ref, a_ref, bw_ref, bs_ref, ba_ref, send, recv, local):
    sky = lax.axis_index("sky")
    band = lax.axis_index("band")
    home_sky, home_band = home_of(sky)
    stays = (home_sky == sky) & (home_band == band)
    is_home, my_tile = tile_at(sky, band)
    pairs = ((w_ref, bw_ref), (s_ref, bs_ref), (a_ref, ba_ref))

    def remote(i, slot):
        src, dst = pairs[i]
        return pltpu.make_async_remote_copy(
            src_ref=src,
            dst_ref=dst.at[slot],
            send_sem=send.at[i],
            recv_sem=recv.at[slot, i],
            device_id=(home_sky, home_band),
            device_id_type=MESH,
        )

    @pl.when(jnp.logical_not(stays))
    def _():
        for i in range(3):
            remote(i, band).start()

    @pl.when(stays)
    def _():
        for i in range(3):
            pltpu.make_async_copy(pairs[i][0], pairs[i][1].at[band], local.at[i]).start()
        for i in range(3):
            pltpu.make_async_copy(pairs[i][0], pairs[i][1].at[band], local.at[i]).wait()

    @pl.when(jnp.logical_not(stays))
    def _():
        for i in range(3):
            remote(i, band).wait_send()

    for slot in range(BANDS):
        own = (my_tile == sky) & (band == slot)

        @pl.when(is_home & jnp.logical_not(own))
        def _():
            for i in range(3):
                remote(i, slot).wait_recv()


def ship(w, s, a):
    vmem = pl.BlockSpec(memory_space=pltpu.VMEM)
    return pl.pallas_call(
        ship_kernel,
        out_shape=(
            jax.ShapeDtypeStruct((BANDS, OBS, STARS), F32),
            jax.ShapeDtypeStruct((BANDS, OBS, STARS), jnp.int32),
            jax.ShapeDtypeStruct((BANDS, BLOCKS, A_END), F32),
        ),
        in_specs=[vmem] * 3,
        out_specs=(vmem,) * 3,
        scratch_shapes=[
            pltpu.SemaphoreType.DMA((3,)),
            pltpu.SemaphoreType.DMA((BANDS, 3)),
            pltpu.SemaphoreType.DMA((3,)),
        ],
        compiler_params=pltpu.CompilerParams(has_side_effects=True),
        name="ship",
    )(w, s, a)


def block_maps(a_ref, blk):
    col = as_column(a_ref[0, blk : blk + 1, A_BF : A_BF + 128], 128)
    row_band = iota((128, 128), 0) // LIST
    lane_band = iota((128, 128), 1) // OWN
    parts = []
    for q in range(6):
        near = a_ref[0, q : q + 1, A_NF : A_NF + 128]
        hit = (col == near) & (row_band == lane_band + 2 * (q % 2))
        parts.append(jnp.where(hit, 1.0, 0.0))
    return parts


def split3(x):
    hi = x.astype(BF16)
    rest = x - hi.astype(F32)
    mid = rest.astype(BF16)
    low = (rest - mid.astype(F32)).astype(BF16)
    return hi, mid, low


def build_kernel(mix_ref, w_ref, s_ref, a_ref, mt_ref, td_ref, u_ref, r_ref):
    row_band = iota((128, 128), 0) // LIST
    lane_band = iota((128, 128), 1) // LIST
    mix = jnp.zeros((128, 128), F32)
    for b2 in range(BANDS):
        for b in range(BANDS):
            mix = jnp.where((row_band == b2) & (lane_band == b), mix_ref[b, b2], mix)
    lane_row = iota((1, 128), 1) // LIST
    entries = iota((LIST, ROWS), 0)
    td_acc = [jnp.zeros((8, 128), F32) for _ in range(6)]
    for blk in range(BLOCKS):
        cols = slice(blk * ROWS, (blk + 1) * ROWS)
        wide, scaled, mean0 = [], [], []
        for b in range(BANDS):
            acc = jnp.zeros((LIST, ROWS), F32)
            star_w = jnp.zeros((1, ROWS), F32)
            for k in range(OBS):
                wk = w_ref[b, k : k + 1, cols]
                acc = acc + jnp.where(s_ref[b, k : k + 1, cols] == entries, wk, 0.0)
                star_w = star_w + wk
            wide.append(acc)
            scaled.append(acc / star_w)
            mean0.append(a_ref[b, blk : blk + 1, A_MEAN : A_MEAN + ROWS])
        pred0 = []
        for b in range(BANDS):
            total = mix_ref[b, 0] * mean0[0]
            for b2 in range(1, BANDS):
                total = total + mix_ref[b, b2] * mean0[b2]
            pred0.append(total)
        w_all = jnp.concatenate(wide, axis=0)
        u_all = jnp.concatenate(scaled, axis=0)
        u_ref[blk] = u_all
        extra = jnp.concatenate(
            pred0 + [jnp.ones((1, ROWS), F32), jnp.zeros((3, ROWS), F32)], axis=0
        )
        dims = (((1,), (1,)), ((), ()))
        gt = lax.dot_general(u_all, w_all, dims, precision=HIGH, preferred_element_type=F32)
        ex = lax.dot_general(extra, w_all, dims, precision=HIGH, preferred_element_type=F32)
        gt = gt * mix
        known = jnp.zeros((1, 128), F32)
        for b in range(BANDS):
            known = known + a_ref[b, blk : blk + 1, A_P : A_P + 128]
            known = known - jnp.where(lane_row == b, ex[b : b + 1, :], 0.0)
        dens = ex[BANDS : BANDS + 1, :]
        maps = [m.astype(BF16) for m in block_maps(a_ref, blk)]
        td = jnp.concatenate([*split3(known), *split3(dens), jnp.zeros((2, 128), BF16)], axis=0)
        parts = split3(gt)
        for q in range(6):
            td_acc[q] = td_acc[q] + jnp.dot(td, maps[q], preferred_element_type=F32)
            for i in range(3):
                moved = jnp.dot(parts[i], maps[q], preferred_element_type=F32).astype(BF16)
                for b2 in range(BANDS):
                    r_ref[i, b2, blk * LIST : (blk + 1) * LIST, q * 128 : (q + 1) * 128] = moved[
                        b2 * LIST : (b2 + 1) * LIST, :
                    ]
    for q in range(6):
        acc = td_acc[q]
        td_ref[0, q : q + 1, :] = acc[0:1] + acc[1:2] + acc[2:3]
        td_ref[1, q : q + 1, :] = acc[3:4] + acc[4:5] + acc[5:6]
    td_ref[:, 6:8, :] = jnp.zeros((2, 2, 128), F32)
    list_row = [a_ref[0, 6 + h : 7 + h, A_NF : A_NF + 128] for h in range(2)]
    pick = []
    for tr in range(3):
        col = as_column(a_ref[0, 2 * tr : 2 * tr + 1, A_NF : A_NF + 128], OWN)
        pick.append(
            jnp.concatenate([jnp.where(col == row, 1.0, 0.0) for row in list_row], axis=1)
        )
    pick = jnp.concatenate(pick, axis=0).astype(BF16)
    for b2 in range(BANDS):
        total = jnp.dot(pick, r_ref[0, b2], preferred_element_type=F32)
        total = total + jnp.dot(pick, r_ref[1, b2], preferred_element_type=F32)
        total = total + jnp.dot(pick, r_ref[2, b2], preferred_element_type=F32)
        mt_ref[b2 * NEAR : (b2 + 1) * NEAR, :] = total


def build(mixing, bw, bs, ba):
    vmem = pl.BlockSpec(memory_space=pltpu.VMEM)
    return pl.pallas_call(
        build_kernel,
        out_shape=(
            jax.ShapeDtypeStruct((WIDE, WIDE), F32),
            jax.ShapeDtypeStruct((2, 8, 128), F32),
            jax.ShapeDtypeStruct((BLOCKS, 128, ROWS), F32),
        ),
        in_specs=[pl.BlockSpec(memory_space=pltpu.SMEM), vmem, vmem, vmem],
        out_specs=(vmem,) * 3,
        scratch_shapes=[pltpu.VMEM((3, BANDS, BLOCKS * LIST, WIDE), BF16)],
        name="build",
    )(mixing, bw, bs, ba)


def sweep_kernel(
    mt_ref, td_ref, a_ref, zs_ref, first_out, first_in, out_buf, in_buf,
    first_send, first_recv, send, recv,
):
    sky = lax.axis_index("sky")
    band = lax.axis_index("band")
    is_home, tile = tile_at(sky, band)
    places = [home_of((tile + d + TILES) % TILES) for d in (1, -1, 2, -2)]

    def first_copy(slot, i):
        return pltpu.make_async_remote_copy(
            src_ref=first_out.at[i],
            dst_ref=first_in.at[i, slot],
            send_sem=first_send.at[i, slot],
            recv_sem=first_recv.at[i, slot],
            device_id=places[slot],
            device_id_type=MESH,
        )

    def step_copy(slot, p):
        return pltpu.make_async_remote_copy(
            src_ref=out_buf.at[p],
            dst_ref=in_buf.at[p, slot],
            send_sem=send.at[p, slot],
            recv_sem=recv.at[p, slot],
            device_id=places[slot],
            device_id_type=MESH,
        )

    def combine(own, got):
        below, above, far_below, far_above = range(4)
        low = [own[q] + got(below, q + 2) + got(far_below, q + 4) for q in (0, 1)]
        mid = [own[q] + got(below, q + 2) + got(above, q - 2) for q in (2, 3)]
        top = [own[q] + got(above, q - 2) + got(far_above, q - 4) for q in (4, 5)]
        return low + mid + top

    eye = iota((128, 128), 0) == iota((128, 128), 1)

    def apply_operator(z):
        acc = jnp.zeros((8, WIDE), F32)
        for r in range(6):
            full = jnp.where(eye, jnp.broadcast_to(z[r], (128, 128)), 0.0)
            col = jnp.sum(full, axis=1, keepdims=True)
            for half in range(2):
                b = (r % 2) * 2 + half
                base = b * NEAR + (r // 2) * OWN
                for i in range(0, OWN, 8):
                    at = half * OWN + i
                    acc = acc + mt_ref[base + i : base + i + 8, :] * col[at : at + 8, :]
        flat = jnp.sum(acc, axis=0, keepdims=True)
        return [flat[:, q * 128 : (q + 1) * 128] for q in range(6)]

    @pl.when(is_home)
    def _():
        for i in range(2):
            for q in range(6):
                first_out[i, q] = td_ref[i, q : q + 1, :]
        for i in range(2):
            for slot in range(4):
                first_copy(slot, i).start()
        for i in range(2):
            for slot in range(4):
                first_copy(slot, i).wait()
        known = combine([first_out[0, q] for q in range(6)], lambda s, q: first_in[0, s, q])
        dens = combine([first_out[1, q] for q in range(6)], lambda s, q: first_in[1, s, q])
        dens = [d + PRIOR_WEIGHT for d in dens]
        colors = [a_ref[0, q : q + 1, A_COL : A_COL + 128] for q in range(6)]
        zero = jnp.zeros((1, 128), F32)
        z0 = tuple(jnp.where(colors[q] == 0.0, known[q] / dens[q], zero) for q in range(6))

        def step(s, z):
            p = s % 2
            color = s % COLORS
            own = apply_operator(z)
            for q in range(6):
                out_buf[p, q] = own[q]
            for slot in range(4):
                step_copy(slot, p).start()
            for slot in range(4):
                step_copy(slot, p).wait()
            pulled = combine(own, lambda i, q: in_buf[p, i, q])
            z = tuple(
                jnp.where(
                    colors[q] == color.astype(F32), (known[q] + pulled[q]) / dens[q], z[q]
                )
                for q in range(6)
            )

            @pl.when(color == COLORS - 1)
            def _():
                for q in range(6):
                    zs_ref[s // COLORS, q] = z[q]

            return z

        lax.fori_loop(1, STEPS, step, z0)


def sweeps(mt, td, ba):
    vmem = pl.BlockSpec(memory_space=pltpu.VMEM)
    return pl.pallas_call(
        sweep_kernel,
        out_shape=jax.ShapeDtypeStruct((SWEEPS, 6, 1, 128), F32),
        in_specs=[vmem] * 3,
        out_specs=vmem,
        scratch_shapes=[
            pltpu.VMEM((2, 6, 1, 128), F32),
            pltpu.VMEM((2, 4, 6, 1, 128), F32),
            pltpu.VMEM((2, 6, 1, 128), F32),
            pltpu.VMEM((2, 4, 6, 1, 128), F32),
            pltpu.SemaphoreType.DMA((2, 4)),
            pltpu.SemaphoreType.DMA((2, 4)),
            pltpu.SemaphoreType.DMA((2, 4)),
            pltpu.SemaphoreType.DMA((2, 4)),
        ],
        compiler_params=pltpu.CompilerParams(has_side_effects=True),
        name="sweeps",
    )(mt, td, ba)


def finish_kernel(mix_ref, zs_ref, a_ref, u_ref, fin_ref):
    lane_band = iota((1, 128), 1) // LIST
    rows_mix, rows_one = [], []
    for b in range(BANDS):
        row = jnp.zeros((1, 128), F32)
        for b2 in range(BANDS):
            row = jnp.where(lane_band == b2, mix_ref[b, b2], row)
        rows_mix.append(row)
        rows_one.append(jnp.where(lane_band == b, 1.0, 0.0))
    snap = [
        jnp.concatenate([zs_ref[n, q] for n in range(SWEEPS)] + [jnp.zeros((4, 128), F32)], axis=0)
        for q in range(6)
    ]
    for blk in range(BLOCKS):
        cols = slice(blk * ROWS, (blk + 1) * ROWS)
        maps = block_maps(a_ref, blk)
        listed = jnp.zeros((8, 128), F32)
        for q in range(6):
            listed = listed + lax.dot_general(
                snap[q], maps[q], (((1,), (1,)), ((), ())), precision=HIGH,
                preferred_element_type=F32,
            )
        lhs = [listed[n : n + 1] * rows_mix[b] for n in range(SWEEPS) for b in range(BANDS)]
        lhs += [listed[SWEEPS - 1 : SWEEPS] * rows_one[b] for b in range(BANDS)]
        lhs.append(jnp.zeros((4, 128), F32))
        moved = jnp.dot(
            jnp.concatenate(lhs, axis=0), u_ref[blk], precision=HIGH, preferred_element_type=F32
        )
        mean0 = [a_ref[b, blk : blk + 1, A_MEAN : A_MEAN + ROWS] for b in range(BANDS)]
        for b in range(BANDS):
            pred0 = mix_ref[b, 0] * mean0[0]
            for b2 in range(1, BANDS):
                pred0 = pred0 + mix_ref[b, b2] * mean0[b2]
            for n in range(SWEEPS):
                at = n * BANDS + b
                fin_ref[b, n : n + 1, cols] = pred0 - moved[at : at + 1]
                to = ((n % 2) * BLOCKS + blk) * 128
                fin_ref[b, 5 + n // 2 : 6 + n // 2, to : to + 128] = listed[n : n + 1]
            at = SWEEPS * BANDS + b
            fin_ref[b, 4:5, cols] = mean0[b] - moved[at : at + 1]
    for b in range(BANDS):
        fin_ref[b, 7:8, :] = jnp.zeros((1, STARS), F32)
        fin_ref[b, 7:8, 0:128] = zs_ref[SWEEPS - 1, 2 + b // 2]


def finish(mixing, zs, ba, u):
    vmem = pl.BlockSpec(memory_space=pltpu.VMEM)
    return pl.pallas_call(
        finish_kernel,
        out_shape=jax.ShapeDtypeStruct((BANDS, 8, STARS), F32),
        in_specs=[pl.BlockSpec(memory_space=pltpu.SMEM), vmem, vmem, vmem],
        out_specs=vmem,
        name="finish",
    )(mixing, zs, ba, u)


def give_kernel(
    fin_ref, m_ref, w_ref, s_ref, zp_ref, means_ref, mis_ref, got, parts,
    send, recv, local, part_send, part_recv,
):
    sky = lax.axis_index("sky")
    band = lax.axis_index("band")
    home_sky, home_band = home_of(sky)
    is_home, tile = tile_at(sky, band)
    stays = (home_sky == sky) & (home_band == band)

    def copy(slot):
        return pltpu.make_async_remote_copy(
            src_ref=fin_ref.at[slot],
            dst_ref=got,
            send_sem=send.at[slot],
            recv_sem=recv,
            device_id=(tile, slot),
            device_id_type=MESH,
        )

    for slot in range(BANDS):
        own = (tile == sky) & (band == slot)

        @pl.when(is_home & jnp.logical_not(own))
        def _():
            copy(slot).start()

    @pl.when(stays)
    def _():
        mine = pltpu.make_async_copy(fin_ref.at[band], got, local)
        mine.start()
        mine.wait()

    for slot in range(BANDS):
        own = (tile == sky) & (band == slot)

        @pl.when(is_home & jnp.logical_not(own))
        def _():
            copy(slot).wait_send()

    @pl.when(jnp.logical_not(stays))
    def _():
        copy(0).wait_recv()

    means_ref[...] = got[4:5, :]
    pair = got[7:8, 0:128]
    zp_ref[...] = jnp.where(band % 2 == 0, pair[:, 0:OWN], pair[:, OWN : 2 * OWN])
    acc = [jnp.zeros((8, 128), F32) for _ in range(SWEEPS)]
    for blk in range(BLOCKS):
        for half in range(2):
            at = blk * ROWS + half * 128
            m = m_ref[:, at : at + 128]
            w = w_ref[:, at : at + 128]
            idx = s_ref[:, at : at + 128] + band * LIST
            for n in range(SWEEPS):
                to = ((n % 2) * BLOCKS + blk) * 128
                table = jnp.broadcast_to(got[5 + n // 2 : 6 + n // 2, to : to + 128], (8, 128))
                picked = jnp.take_along_axis(table, idx, axis=1)
                left = m - got[n : n + 1, at : at + 128] - picked
                acc[n] = acc[n] + w * left * left
    lane = iota((1, 128), 1)
    row = jnp.zeros((1, 128), F32)
    for n in range(SWEEPS):
        total = jnp.sum(jnp.sum(acc[n], axis=0, keepdims=True), axis=1, keepdims=True)
        row = jnp.where(lane == n, total, row)
    parts[0] = row

    def part(d):
        return pltpu.make_async_remote_copy(
            src_ref=parts.at[0],
            dst_ref=parts.at[d],
            send_sem=part_send,
            recv_sem=part_recv,
            device_id=((sky + TILES - d) % TILES, band),
            device_id_type=MESH,
        )

    def push(d, carry):
        part(d).start()
        return carry

    lax.fori_loop(1, TILES, push, 0)
    everyone = pltpu.make_async_remote_copy(
        src_ref=parts.at[pl.ds(1, TILES - 1)],
        dst_ref=parts.at[pl.ds(1, TILES - 1)],
        send_sem=part_send,
        recv_sem=part_recv,
        device_id=((sky + 1) % TILES, band),
        device_id_type=MESH,
    )
    everyone.wait()
    by_tile = pltpu.roll(parts[...].reshape(TILES, 128), sky, 0)
    mis_ref[...] = jnp.sum(by_tile, axis=0, keepdims=True)


def give_back(fin, m, w, s):
    vmem = pl.BlockSpec(memory_space=pltpu.VMEM)
    return pl.pallas_call(
        give_kernel,
        out_shape=(
            jax.ShapeDtypeStruct((1, OWN), F32),
            jax.ShapeDtypeStruct((1, STARS), F32),
            jax.ShapeDtypeStruct((1, 128), F32),
        ),
        in_specs=[vmem] * 4,
        out_specs=(vmem,) * 3,
        scratch_shapes=[
            pltpu.VMEM((8, STARS), F32),
            pltpu.VMEM((TILES, 1, 128), F32),
            pltpu.SemaphoreType.DMA((BANDS,)),
            pltpu.SemaphoreType.DMA,
            pltpu.SemaphoreType.DMA,
            pltpu.SemaphoreType.DMA,
            pltpu.SemaphoreType.DMA,
        ],
        compiler_params=pltpu.CompilerParams(has_side_effects=True),
        name="give_back",
    )(fin, m, w, s)


def body(magnitudes, weights, slots, block_fields, owner, colors, color_terms):
    my_tile = lax.axis_index("sky")
    my_band = lax.axis_index("band")
    m, w, s = magnitudes[0], weights[0], slots[0]
    fields = owner.shape[0]
    mixing = (
        jnp.eye(BANDS, dtype=F32) + color_terms - jnp.diag(jnp.sum(color_terms, axis=1))
    )
    mean0 = (jnp.sum(w * m, axis=0) / jnp.sum(w, axis=0)).reshape(BLOCKS, ROWS)
    grid = (w * m).reshape(OBS, BLOCKS, 1, ROWS)
    hits = s.reshape(OBS, BLOCKS, 1, ROWS) == jnp.arange(LIST, dtype=jnp.int32)[None, None, :, None]
    sums = jnp.sum(jnp.where(hits, grid, 0.0), axis=(0, 3))
    lane_band = jnp.arange(128, dtype=jnp.int32) // LIST
    sums = jnp.where(lane_band[None] == my_band, jnp.tile(sums, (1, BANDS)), 0.0)
    listed = block_fields.astype(F32)
    order = jnp.sort(owner * fields + jnp.arange(fields, dtype=jnp.int32)) % fields
    nearby = jnp.mod(my_tile + jnp.arange(3, dtype=jnp.int32) - 1, TILES)
    near = jnp.take(order.reshape(TILES, OWN), nearby, axis=0)
    near_colors = jnp.take(colors, near)

    def per_band(values):
        return jnp.tile(values.astype(F32)[:, None, None, :], (1, 2, 2, 1)).reshape(6, 128)

    lists = jnp.concatenate([per_band(near), listed.reshape(2, 128)], axis=0)
    cols = jnp.concatenate([per_band(near_colors), jnp.zeros((2, 128), F32)], axis=0)
    table = jnp.concatenate([mean0, sums, jnp.tile(listed, (1, BANDS)), lists, cols], axis=1)
    bw, bs, ba = ship(w, s, table)
    mt, td, u = build(mixing, bw, bs, ba)
    zs = sweeps(mt, td, ba)
    fin = finish(mixing, zs, ba, u)
    zp, means, mis = give_back(fin, m, w, s)
    misfit = mis[:, :SWEEPS] / (OBS * STARS * TILES)
    return zp, means, misfit.reshape(SWEEPS, 1)


def solution(mesh):
    in_specs = (
        P("band", None, "sky"),
        P("band", None, "sky"),
        P("band", None, "sky"),
        P("sky", None),
        P(),
        P(),
        P(),
    )
    out_specs = (P("band", "sky"), P("band", "sky"), P(None, "band"))
    return jax.shard_map(body, mesh=mesh, in_specs=in_specs, out_specs=out_specs, check_vma=False)
```

time: 717 us -> 191 us (0.27)
  the two profiles are of different devices: /device:TPU:2 before, /device:TPU:1 now
where the time goes in v1:
time: 191 us
  Pallas kernels  172 us (90%)
  other arithmetic  11.9 us (6%)
  local copies, waits for them, and re-layouts  5.76 us (3%)
    pallas_call x1, Pallas kernels, sweeps(): pl.pallas_call(sweep_kernel, out_shape=jax.ShapeDtypeStruct((SWEEPS, 6, 1...  95.4 us
    pallas_call x1, Pallas kernels, ship(): pl.pallas_call(ship_kernel, out_shape=(jax.ShapeDtypeStruct((BANDS, OBS,...  28.5 us
    pallas_call x1, Pallas kernels, give_back(): pl.pallas_call(give_kernel, out_shape=(jax.ShapeDtypeStruct((1, OWN), F32...  25.9 us
    pallas_call x1, Pallas kernels, finish(): pl.pallas_call(finish_kernel, out_shape=jax.ShapeDtypeStruct((BANDS, 8, S...  13.6 us
    pallas_call x1, Pallas kernels, build(): pl.pallas_call(build_kernel, out_shape=(jax.ShapeDtypeStruct((WIDE, WIDE)...  8.69 us
    sort x1, other arithmetic, body(): jnp.sort(owner * fields + jnp.arange(fields, dtype=jnp.int32)) % fields  5.76 us

profile of v1, /device:TPU:1, one launch (start us, length us, event | category | flops | bytes accessed | tf_op | source)
XLA Modules:
  0.0 190.6 jit_solution(1266499077594607078)
XLA Ops:
  0.6 0.0 copy-start
  0.6 0.0 copy-start.1
  0.7 0.0 copy-start.2
  0.7 0.0 copy-start.3
  0.7 0.8 reduce_sum.36
  1.5 1.3 select_subtract_fusion.mix_ref
  2.9 0.7 convert_element_type.21
  3.6 0.1 reshape.199
  3.6 0.9 multiply_reduce_fusion
  4.6 0.1 tile.35
  4.6 0.7 iota_add_fusion
  5.4 5.8 %sort.15 = (s32[4096]{0:T(1024)S(1)}, s32[4096]{0:T(1024)}) sort(s32[4096]{0:T(1024)S(1)} %iota_add_fusion, s32[4096]{0:T(1024)S(1)} %iota.48), dimensions={0}, to_apply=%region_4.5 | sort | flops 49152 | bytes 65536 | tf_op jit(solution)/shard_map/jit(sort)/sort | solution.py:554
  11.1 0.1 reshape.198
  11.2 0.6 gather_fusion
  11.8 0.1 compare_select_fusion
  11.9 0.1 reshape.211
  12.0 1.4 gather_fusion.1
  13.4 0.1 reshape.210
  13.5 0.1 select_convert_fusion
  13.6 0.1 tile.39
  13.6 0.1 tile.37
  13.8 0.4 select_reduce_fusion
  14.2 0.1 tile.33
  14.4 0.6 copy-done.4
  14.9 28.5 %ship.1 = (f32[4,8,2048]{2,1,0:T(8,128)}, s32[4,8,2048]{2,1,0:T(8,128)}, f32[4,8,768]{2,1,0:T(8,128)}) custom-call(f32[8,2048]{1,0:T(8,128)} %bitcast.21, s32[8,2048]{1,0:T(8,128)} %bitcast.24, f32[8,768]{1,0:T(8,128)} %copy-done.4), custom_call_target="tpu_custom_call" | custom-call | tf_op jit(solution)/shard_map/ship/pallas_call | solution.py:113
  43.4 8.7 %build.1 = (f32[768,768]{1,0:T(8,128)}, f32[2,8,128]{2,1,0:T(8,128)}, f32[8,128,256]{2,1,0:T(8,128)}) custom-call(f32[4,4]{1,0:T(4,128)} %select_subtract_fusion.mix_ref, f32[4,8,2048]{2,1,0:T(8,128)} %get-tuple-element.15.w_ref, s32[4,8,2048]{2,1,0:T(8,128)} %get-tuple-element.16.s_ref, f32[4,8,768]{2,1,0:T(8,128)} %get-tuple-element.17.a_ref), custom_call_target="tpu_custom_call" | custom-call | tf_op jit(solution)/shard_map/build/pallas_call | solution.py:229
  52.1 95.4 %sweeps.1.zs_ref = f32[4,6,1,128]{3,2,1,0:T(1,128)} custom-call(f32[768,768]{1,0:T(8,128)} %get-tuple-element.18.mt_ref, f32[2,8,128]{2,1,0:T(8,128)} %get-tuple-element.19.td_ref, f32[4,8,768]{2,1,0:T(8,128)} %get-tuple-element.17.a_ref), custom_call_target="tpu_custom_call" | custom-call | tf_op jit(solution)/shard_map/sweeps/pallas_call | solution.py:343
  147.5 13.6 %finish.1.fin_ref = f32[4,8,2048]{2,1,0:T(8,128)} custom-call(f32[4,4]{1,0:T(4,128)} %select_subtract_fusion.mix_ref, f32[4,6,1,128]{3,2,1,0:T(1,128)} %sweeps.1.zs_ref, f32[4,8,768]{2,1,0:T(8,128)} %get-tuple-element.17.a_ref, f32[8,128,256]{2,1,0:T(8,128)} %get-tuple-element.20.u_ref), custom_call_target="tpu_custom_call" | custom-call | tf_op jit(solution)/shard_map/finish/pallas_call | solution.py:410
  161.2 25.9 %give_back.1 = (f32[1,64]{1,0:T(1,128)}, f32[1,2048]{1,0:T(1,128)}, f32[1,128]{1,0:T(1,128)}) custom-call(f32[4,8,2048]{2,1,0:T(8,128)} %finish.1.fin_ref, f32[8,2048]{1,0:T(8,128)} %bitcast.23, f32[8,2048]{1,0:T(8,128)} %bitcast.22, s32[8,2048]{1,0:T(8,128)} %bitcast.25), custom_call_target="tpu_custom_call" | custom-call | tf_op jit(solution)/shard_map/give_back/pallas_call | solution.py:516
  187.1 1.1 multiply_bitcast_fusion
  188.1 1.1 copy.22
  189.3 1.3 copy.23
  (26 shorter events, 0.2 us)
Async XLA Ops:
  0.6 11.3 %copy-start = (s32[4096]{0:T(1024)S(1)}, s32[4096]{0:T(1024)}, u32[]{:S(2)}) copy-start(s32[4096]{0:T(1024)} %param.12) | copy-start | bytes 49156
  0.6 13.1 %copy-start.1 = (f32[1,8,2048]{2,1,0:T(8,128)S(1)}, f32[1,8,2048]{2,1,0:T(8,128)}, u32[]{:S(2)}) copy-start(f32[1,8,2048]{2,1,0:T(8,128)} %param.8) | copy-start | bytes 196612
  0.7 13.1 %copy-start.2 = (f32[1,8,2048]{2,1,0:T(8,128)S(1)}, f32[1,8,2048]{2,1,0:T(8,128)}, u32[]{:S(2)}) copy-start(f32[1,8,2048]{2,1,0:T(8,128)} %param.7) | copy-start | bytes 196612
  0.7 13.1 %copy-start.3 = (s32[1,8,2048]{2,1,0:T(8,128)S(1)}, s32[1,8,2048]{2,1,0:T(8,128)}, u32[]{:S(2)}) copy-start(s32[1,8,2048]{2,1,0:T(8,128)} %param.9) | copy-start | bytes 196612
  14.3 0.6 copy-start.4

commit v2 on v0

v2 whole, which is shorter than its diff:
```python
import functools

import jax
import jax.numpy as jnp
from jax import lax
from jax.experimental import pallas as pl
from jax.experimental.pallas import tpu as pltpu
from jax.sharding import PartitionSpec as P

COLORS = 8
SWEEPS = 4
PRIOR_WEIGHT = 1.0

TILES = 64
BANDS = 4
OBS = 8
BLOCKS = 8
ROWS = 256
STARS = BLOCKS * ROWS
LIST = 32
OWN = 64
NEAR = 3 * OWN
CHUNKS = 4
PER = BLOCKS // CHUNKS
SPAN = PER * ROWS
WIDE = BANDS * NEAR
STEPS = COLORS * SWEEPS
MESH = pl.DeviceIdType.MESH
HIGH = lax.Precision.HIGHEST
F32 = jnp.float32
BF16 = jnp.bfloat16


def home_of(tile):
    half = tile // 32
    row = tile // 8
    y = row % 4
    z = tile % 8
    leg = z // 4
    y_new = y + half * (3 - 2 * y)
    z_new = z + leg * (7 - 2 * z)
    x_lo = (1 - half + row + leg) % 2
    return half * 32 + y_new * 8 + z_new, x_lo * 2 + 1


def tile_at(sky, band):
    half = sky // 32
    y_new = (sky // 8) % 4
    z_new = sky % 8
    y = y_new + half * (3 - 2 * y_new)
    row = half * 4 + y
    leg = (band // 2 + 1 + half + row) % 2
    z = z_new + leg * (7 - 2 * z_new)
    is_home = (band % 2 == 1) & (z_new < 4)
    return is_home, (row * 8 + z) % TILES


def iota(shape, dim):
    return lax.broadcasted_iota(jnp.int32, shape, dim)


def as_column(row, count):
    eye = iota((count, 128), 0) == iota((count, 128), 1)
    full = jnp.broadcast_to(row, (count, 128))
    return jnp.sum(jnp.where(eye, full, 0.0), axis=1, keepdims=True)


def as_row(col, shift):
    n = col.shape[0]
    hit = iota((n, 128), 1) == iota((n, 128), 0) + shift
    return jnp.sum(jnp.where(hit, col, 0.0), axis=0, keepdims=True)


def split(x, terms):
    parts = []
    for _ in range(terms - 1):
        part = x.astype(BF16)
        parts.append(part)
        x = x - part.astype(F32)
    return parts + [x.astype(BF16)]


def tile_tables(tile, own_ref, col_ref, lst_ref, near_ref):
    rows = own_ref.shape[0]
    until = jnp.where(iota((128, 128), 0) <= iota((128, 128), 1), 1.0, 0.0).astype(BF16)
    before = jnp.where(iota((rows, rows), 1) < iota((rows, rows), 0), 1.0, 0.0).astype(BF16)
    number = (iota((rows, 128), 0) * 128 + iota((rows, 128), 1)).astype(F32)
    shade = col_ref[...].astype(F32)
    rank_at = iota((OWN, 128), 0).astype(F32)
    for tr in range(3):
        mine = own_ref[...] == (tile + tr - 1 + TILES) % TILES
        one = jnp.where(mine, 1.0, 0.0)
        inside = jnp.dot(one.astype(BF16), until, preferred_element_type=F32)
        above = jnp.dot(before, one.astype(BF16), preferred_element_type=F32)
        above = jnp.sum(above, axis=1, keepdims=True)
        rank = jnp.where(mine, inside + above - 1.0, -1.0)
        ids = jnp.zeros((OWN, 128), F32)
        cols = jnp.zeros((OWN, 128), F32)
        for i in range(rows):
            hit = rank[i : i + 1] == rank_at
            ids = ids + jnp.where(hit, number[i : i + 1], 0.0)
            cols = cols + jnp.where(hit, shade[i : i + 1], 0.0)
        for value, at in ((ids, 0), (cols, 128)):
            col = jnp.sum(value, axis=1, keepdims=True)
            row = as_row(col, 0) + as_row(col, OWN)
            near_ref[2 * tr : 2 * tr + 1, at : at + 128] = row
            near_ref[2 * tr + 1 : 2 * tr + 2, at : at + 128] = row
    near_ref[6:8, 128:256] = jnp.zeros((2, 128), F32)
    near_ref[6:8, 0:128] = lst_ref[0:2, 0:128].astype(F32)
    near_ref[:, 256:384] = lst_ref[2:10, 0:128].astype(F32)


def star_tables(m_ref, w_ref, s_ref, aux_ref):
    entries = iota((LIST, ROWS), 0)
    sums = [jnp.zeros((1, 128), F32) for _ in range(2)]
    for blk in range(BLOCKS):
        cols = slice(blk * ROWS, (blk + 1) * ROWS)
        acc = jnp.zeros((LIST, ROWS), F32)
        for k in range(OBS):
            value = w_ref[k : k + 1, cols] * m_ref[k : k + 1, cols]
            acc = acc + jnp.where(s_ref[k : k + 1, cols] == entries, value, 0.0)
        top = jnp.sum(w_ref[:, cols] * m_ref[:, cols], axis=0, keepdims=True)
        aux_ref[blk : blk + 1, 0:ROWS] = top / jnp.sum(w_ref[:, cols], axis=0, keepdims=True)
        col = jnp.sum(acc, axis=1, keepdims=True)
        sums[blk // 4] = sums[blk // 4] + as_row(col, (blk % 4) * LIST)
    aux_ref[2:8, 256:384] = jnp.zeros((6, 128), F32)
    for h in range(2):
        aux_ref[h : h + 1, 256:384] = sums[h]


def solve_kernel(
    ct_ref, m_ref, w_ref, s_ref, own_ref, col_ref, lst_ref,
    out_ref, means_ref,
    aux, near, bw, bs, ba, bn, u_ref, r_ref, mt_ref, pick2_ref,
    first_out, first_in, out_buf, in_buf, fin, fin_means, got, got_means, parts,
    ship_send, ship_recv, tab_send, tab_recv, local,
    first_send, first_recv, send, recv,
    fin_send, fin_recv, mean_send, mean_recv, part_send, part_recv,
):
    sky = lax.axis_index("sky")
    band = lax.axis_index("band")
    home_sky, home_band = home_of(sky)
    stays = (home_sky == sky) & (home_band == band)
    moves = jnp.logical_not(stays)
    is_home, tile = tile_at(sky, band)
    places = [home_of((tile + d + TILES) % TILES) for d in (1, -1, 2, -2)]

    def owns(slot):
        return (tile == sky) & (band == slot)

    barrier = pltpu.get_barrier_semaphore()

    @pl.when(moves)
    def _():
        pl.semaphore_signal(barrier, inc=1, device_id=(home_sky, home_band), device_id_type=MESH)

    @pl.when(is_home)
    def _():
        for place in places:
            pl.semaphore_signal(barrier, inc=1, device_id=place, device_id_type=MESH)
        for slot in range(BANDS):

            @pl.when(jnp.logical_not(owns(slot)))
            def _():
                pl.semaphore_signal(barrier, inc=1, device_id=(tile, slot), device_id_type=MESH)

    star_tables(m_ref, w_ref, s_ref, aux)
    tile_tables(sky, own_ref, col_ref, lst_ref, near)

    @pl.when(is_home & moves)
    def _():
        pl.semaphore_wait(barrier, 9)

    @pl.when(is_home & stays)
    def _():
        pl.semaphore_wait(barrier, 7)

    @pl.when(jnp.logical_not(is_home))
    def _():
        pl.semaphore_wait(barrier, 1)

    def chunk(ref, slot, c):
        at = pl.ds(c * SPAN, SPAN)
        return ref.at[:, at] if slot is None else ref.at[slot, :, at]

    def ship_copy(i, slot, c):
        src, dst = ((w_ref, bw), (s_ref, bs))[i]
        return pltpu.make_async_remote_copy(
            src_ref=chunk(src, None, c),
            dst_ref=chunk(dst, slot, c),
            send_sem=ship_send.at[i, c],
            recv_sem=ship_recv.at[slot, i, c],
            device_id=(home_sky, home_band),
            device_id_type=MESH,
        )

    def table_copy(i, slot):
        src, dst = ((aux, ba.at[slot]), (near, bn))[i]
        return pltpu.make_async_remote_copy(
            src_ref=src,
            dst_ref=dst,
            send_sem=tab_send.at[i],
            recv_sem=tab_recv.at[slot, i],
            device_id=(home_sky, home_band),
            device_id_type=MESH,
        )

    teller = 0

    @pl.when(moves)
    def _():
        @pl.when(band == teller)
        def _():
            table_copy(1, band).start()

        table_copy(0, band).start()
        for c in range(CHUNKS):
            for i in range(2):
                ship_copy(i, band, c).start()

    @pl.when(stays)
    def _():
        copies = [
            pltpu.make_async_copy(aux, ba.at[band], local.at[0]),
            pltpu.make_async_copy(w_ref, bw.at[band], local.at[1]),
            pltpu.make_async_copy(s_ref, bs.at[band], local.at[2]),
        ]
        for copy in copies:
            copy.start()
        for copy in copies:
            copy.wait()

    mix = []
    for b in range(BANDS):
        total = ct_ref[b, 0]
        for b2 in range(1, BANDS):
            total = total + ct_ref[b, b2]
        mix.append([ct_ref[b, b2] + (1.0 - total if b == b2 else 0.0) for b2 in range(BANDS)])

    def await_tables():
        table_copy(1, teller).wait_recv()
        for slot in range(BANDS):

            @pl.when(jnp.logical_not(owns(slot)))
            def _():
                table_copy(0, slot).wait_recv()

    def await_chunk(c):
        for slot in range(BANDS):

            @pl.when(jnp.logical_not(owns(slot)))
            def _():
                for i in range(2):
                    ship_copy(i, slot, c).wait_recv()

    def build():
        row_band = iota((128, 128), 0) // LIST
        lane_list = iota((128, 128), 1) // LIST
        lane_own = iota((128, 128), 1) // OWN
        mixes = jnp.zeros((128, 128), F32)
        for b2 in range(BANDS):
            for b in range(BANDS):
                mixes = jnp.where((row_band == b2) & (lane_list == b), mix[b][b2], mixes)
        entries = iota((LIST, ROWS), 0)
        await_tables()
        known = [[ba[b, h : h + 1, 256:384] for h in range(2)] for b in range(BANDS)]
        dens = [[jnp.zeros((1, 128), F32) for _ in range(2)] for _ in range(BANDS)]
        for blk in range(BLOCKS):
            if blk % PER == 0:
                await_chunk(blk // PER)
            cols = slice(blk * ROWS, (blk + 1) * ROWS)
            wide, scaled = [], []
            mean0 = [ba[b, blk : blk + 1, 0:ROWS] for b in range(BANDS)]
            for b in range(BANDS):
                acc = jnp.zeros((LIST, ROWS), F32)
                for k in range(OBS):
                    wk = bw[b, k : k + 1, cols]
                    acc = acc + jnp.where(bs[b, k : k + 1, cols] == entries, wk, 0.0)
                star_w = jnp.sum(bw[b, :, cols], axis=0, keepdims=True)
                wide.append(acc)
                scaled.append(acc * (1.0 / star_w))
                u_ref[b, blk * LIST : (blk + 1) * LIST, :] = scaled[b]
                pred0 = mix[b][0] * mean0[0]
                for b2 in range(1, BANDS):
                    pred0 = pred0 + mix[b][b2] * mean0[b2]
                h, at = blk // 4, (blk % 4) * LIST
                pulled = jnp.sum(acc * pred0, axis=1, keepdims=True)
                known[b][h] = known[b][h] - as_row(pulled, at)
                dens[b][h] = dens[b][h] + as_row(jnp.sum(acc, axis=1, keepdims=True), at)
            w_hi, w_lo = split(jnp.concatenate(wide, axis=0), 2)
            u_hi, u_lo = split(jnp.concatenate(scaled, axis=0), 2)
            dims = (((1,), (1,)), ((), ()))
            both = lax.dot_general(
                jnp.concatenate([u_hi, u_lo], axis=0), w_hi, dims, preferred_element_type=F32
            )
            gt = both[0:128] + both[128:256]
            gt = gt + lax.dot_general(u_hi, w_lo, dims, preferred_element_type=F32)
            lhs = jnp.concatenate(split(gt * mixes, 2), axis=0)
            col = as_column(bn[blk : blk + 1, 256:384], 128)
            for q in range(6):
                hit = (col == bn[q : q + 1, 0:128]) & (row_band == lane_own + 2 * (q % 2))
                moved = jnp.dot(
                    lhs, jnp.where(hit, 1.0, 0.0).astype(BF16), preferred_element_type=F32
                ).astype(BF16)
                for i in range(2):
                    for b2 in range(BANDS):
                        at = i * 128 + b2 * LIST
                        r_ref[
                            i, b2, blk * LIST : (blk + 1) * LIST, q * 128 : (q + 1) * 128
                        ] = moved[at : at + LIST]
        pick = []
        for tr in range(3):
            col = as_column(bn[2 * tr : 2 * tr + 1, 0:128], OWN)
            one = jnp.concatenate(
                [jnp.where(col == bn[6 + h : 7 + h, 0:128], 1.0, 0.0) for h in range(2)], axis=1
            ).astype(BF16)
            none = jnp.zeros((OWN, 256), BF16)
            pick2_ref[tr, 0:OWN, 0:256] = one
            pick2_ref[tr, OWN:128, 0:256] = none
            pick2_ref[tr, 0:OWN, 256:512] = none
            pick2_ref[tr, OWN:128, 256:512] = one
            pick.append(one)
        pick = jnp.concatenate(pick, axis=0)
        rows = [jnp.concatenate(known[b], axis=1) for b in range(BANDS)]
        rows += [jnp.concatenate(dens[b], axis=1) for b in range(BANDS)]
        terms = jnp.concatenate(split(jnp.concatenate(rows, axis=0), 3), axis=0)
        sums = lax.dot_general(terms, pick, (((1,), (1,)), ((), ())), preferred_element_type=F32)
        sums = sums[0:8] + sums[8:16] + sums[16:24]
        for i in range(2):
            for q in range(6):
                tr, b = q // 2, 2 * (q % 2)
                at = slice(tr * OWN, (tr + 1) * OWN)
                low, high = i * BANDS + b, i * BANDS + b + 1
                first_out[i, q] = jnp.concatenate(
                    [sums[low : low + 1, at], sums[high : high + 1, at]], axis=1
                )
        for i in range(2):
            for slot in range(4):
                first_copy(slot, i).start()
        for b2 in range(BANDS):
            total = jnp.dot(pick, r_ref[0, b2], preferred_element_type=F32)
            total = total + jnp.dot(pick, r_ref[1, b2], preferred_element_type=F32)
            mt_ref[b2 * NEAR : (b2 + 1) * NEAR, :] = total

    def first_copy(slot, i):
        return pltpu.make_async_remote_copy(
            src_ref=first_out.at[i],
            dst_ref=first_in.at[i, slot],
            send_sem=first_send.at[i, slot],
            recv_sem=first_recv.at[i, slot],
            device_id=places[slot],
            device_id_type=MESH,
        )

    part_of = (pl.ds(2, 4), pl.ds(0, 4), pl.ds(4, 2), pl.ds(0, 2))

    def step_copy(slot, p):
        return pltpu.make_async_remote_copy(
            src_ref=out_buf.at[p, part_of[slot]],
            dst_ref=in_buf.at[p, slot, part_of[slot]],
            send_sem=send.at[p, slot],
            recv_sem=recv.at[p, slot],
            device_id=places[slot],
            device_id_type=MESH,
        )

    below, above, far_below, far_above = range(4)

    def combine_mid(own, got):
        return [own[q] + got(below, q + 2) + got(above, q - 2) for q in (2, 3)]

    def combine_rest(own, got):
        low = [own[q] + got(below, q + 2) + got(far_below, q + 4) for q in (0, 1)]
        top = [own[q] + got(above, q - 2) + got(far_above, q - 4) for q in (4, 5)]
        return low, top

    def columns(row):
        eye = iota((128, 128), 0) == iota((128, 128), 1)
        full = jnp.where(eye, jnp.broadcast_to(row, (128, 128)), 0.0)
        return jnp.sum(full, axis=1, keepdims=True)

    def pull(accs, pieces, cols):
        for r, col in cols.items():
            for half in range(2):
                b = (r % 2) * 2 + half
                base = b * NEAR + (r // 2) * OWN
                for i in range(0, OWN, 8):
                    at = half * OWN + i
                    c = col[at : at + 8, :]
                    for j, q in enumerate(pieces):
                        accs[j] = accs[j] + mt_ref[base + i : base + i + 8, q * 128 : (q + 1) * 128] * c
        return accs

    outer, inner = (0, 1, 4, 5), (2, 3)

    def evaluate(n, z, last):
        zb = [[None, None] for _ in range(BANDS)]
        total = jnp.zeros((8, 512), F32)
        for tr in range(3):
            pair = jnp.concatenate([z[2 * tr], z[2 * tr + 1]], axis=0)
            lhs = jnp.concatenate(split(pair, 3) + [jnp.zeros((2, 128), BF16)], axis=0)
            total = total + jnp.dot(lhs, pick2_ref[tr], preferred_element_type=F32)
        total = total[0:2] + total[2:4] + total[4:6]
        means = []
        for b in range(BANDS):
            rows = []
            for h in range(2):
                at = (b % 2) * 256 + h * 128
                row = total[b // 2 : b // 2 + 1, at : at + 128]
                fin[n, b, h : h + 1, 256:384] = row
                col = columns(row)
                for i in range(4):
                    blk = h * 4 + i
                    value = u_ref[b, blk * LIST : (blk + 1) * LIST, :] * col[i * LIST : (i + 1) * LIST, :]
                    rows.append(jnp.sum(value, axis=0, keepdims=True))
            means.append(ba[b, :, 0:ROWS] - jnp.concatenate(rows, axis=0))
            fin[n, b, 2:3, 256:384] = z[2 + b // 2]
            fin[n, b, 3:8, 256:384] = jnp.zeros((5, 128), F32)
        for b in range(BANDS):
            pred = mix[b][0] * means[0]
            for b2 in range(1, BANDS):
                pred = pred + mix[b][b2] * means[b2]
            fin[n, b, :, 0:ROWS] = pred
            if last:
                fin_means[b] = means[b]
        for slot in range(BANDS):

            @pl.when(jnp.logical_not(owns(slot)))
            def _():
                fin_copy(n, slot).start()
                if last:
                    mean_copy(slot).start()

    def fin_copy(n, slot):
        return pltpu.make_async_remote_copy(
            src_ref=fin.at[n, slot],
            dst_ref=got.at[n],
            send_sem=fin_send.at[n, slot],
            recv_sem=fin_recv.at[n],
            device_id=(tile, slot),
            device_id_type=MESH,
        )

    def mean_copy(slot):
        return pltpu.make_async_remote_copy(
            src_ref=fin_means.at[slot],
            dst_ref=got_means,
            send_sem=mean_send.at[slot],
            recv_sem=mean_recv,
            device_id=(tile, slot),
            device_id_type=MESH,
        )

    @pl.when(is_home)
    def _():
        build()
        for i in range(2):
            for slot in range(4):
                first_copy(slot, i).wait()
        start = []
        for i in range(2):
            own = [first_out[i, q] for q in range(6)]
            low, top = combine_rest(own, lambda s, q: first_in[i, s, q])
            start.append(low + combine_mid(own, lambda s, q: first_in[i, s, q]) + top)
        known, dens = start
        scale = [1.0 / (d + PRIOR_WEIGHT) for d in dens]
        colors = [bn[q : q + 1, 128:256] for q in range(6)]
        zero = jnp.zeros((1, 128), F32)
        z = [jnp.where(colors[q] == 0.0, known[q] * scale[q], zero) for q in range(6)]
        cols = {q: columns(z[q]) for q in range(6)}
        accs = pull([jnp.zeros((8, 128), F32) for _ in range(6)], range(6), cols)
        for q in range(6):
            out_buf[1, q] = jnp.sum(accs[q], axis=0, keepdims=True)
        for slot in (2, 3, 0, 1):
            step_copy(slot, 1).start()

        def renew(q, color, pulled, old):
            return jnp.where(colors[q] == color, (known[q] + pulled) * scale[q], old)

        def absorb(s, z, then):
            p = s % 2
            color = (s % COLORS).astype(F32) if not isinstance(s, int) else float(s % COLORS)
            own = [out_buf[p, q] for q in range(6)]
            take = lambda i, q: in_buf[p, i, q]
            z = list(z)
            for slot in (0, 1):
                step_copy(slot, p).wait_recv()
            mid = combine_mid(own, take)
            for q in inner:
                z[q] = renew(q, color, mid[q - 2], z[q])
            accs = None
            if then:
                cols = {q: columns(z[q]) for q in inner}
                accs = pull([jnp.zeros((8, 128), F32) for _ in range(6)], range(6), cols)
            for slot in (2, 3):
                step_copy(slot, p).wait_recv()
            low, top = combine_rest(own, take)
            for j, q in enumerate(outer):
                z[q] = renew(q, color, (low + top)[j], z[q])
            return z, accs

        def step(s, z):
            p = s % 2

            @pl.when(s % COLORS == 0)
            def _():
                evaluate(s // COLORS - 1, z, False)

            z, accs = absorb(s, z, True)
            cols = {q: columns(z[q]) for q in outer}
            far = pull([accs[q] for q in outer], outer, cols)
            for j, q in enumerate(outer):
                out_buf[1 - p, q] = jnp.sum(far[j], axis=0, keepdims=True)
            for slot in (2, 3):
                step_copy(slot, 1 - p).start()
            near_accs = pull([accs[q] for q in inner], inner, cols)
            for j, q in enumerate(inner):
                out_buf[1 - p, q] = jnp.sum(near_accs[j], axis=0, keepdims=True)
            for slot in (0, 1):
                step_copy(slot, 1 - p).start()
            for slot in range(4):
                step_copy(slot, p).wait_send()
            return tuple(z)

        z = lax.fori_loop(1, STEPS - 1, step, tuple(z))
        z, _ = absorb(STEPS - 1, z, False)
        evaluate(SWEEPS - 1, z, True)
        for slot in range(4):
            step_copy(slot, (STEPS - 1) % 2).wait_send()

    @pl.when(moves)
    def _():
        @pl.when(band == teller)
        def _():
            table_copy(1, band).wait_send()

        table_copy(0, band).wait_send()
        for c in range(CHUNKS):
            for i in range(2):
                ship_copy(i, band, c).wait_send()

    def squares(n):
        @pl.when(moves)
        def _():
            fin_copy(n, 0).wait_recv()

        @pl.when(stays)
        def _():
            mine = pltpu.make_async_copy(fin.at[n, band], got.at[n], local.at[0])
            mine.start()
            mine.wait()

        acc = jnp.zeros((8, 128), F32)
        for blk in range(BLOCKS):
            for half in range(2):
                at = blk * ROWS + half * 128
                table = jnp.broadcast_to(got[n, blk // 4 : blk // 4 + 1, 256:384], (8, 128))
                idx = s_ref[:, at : at + 128] + (blk % 4) * LIST
                picked = jnp.take_along_axis(table, idx, axis=1)
                left = m_ref[:, at : at + 128] - got[n, blk : blk + 1, half * 128 : half * 128 + 128]
                left = left - picked
                acc = acc + w_ref[:, at : at + 128] * left * left
        total = jnp.sum(jnp.sum(acc, axis=0, keepdims=True), axis=1, keepdims=True)
        return jnp.where(iota((1, 128), 1) == n, total, 0.0)

    row = squares(0)
    for n in range(1, SWEEPS):
        row = row + squares(n)
    parts[0] = row

    def part(d):
        return pltpu.make_async_remote_copy(
            src_ref=parts.at[0],
            dst_ref=parts.at[d],
            send_sem=part_send,
            recv_sem=part_recv,
            device_id=((sky + TILES - d) % TILES, band),
            device_id_type=MESH,
        )

    def push(d, carry):
        part(d).start()
        return carry

    lax.fori_loop(1, TILES, push, 0)

    @pl.when(moves)
    def _():
        mean_copy(0).wait_recv()

    @pl.when(stays)
    def _():
        mine = pltpu.make_async_copy(fin_means.at[band], got_means, local.at[1])
        mine.start()
        mine.wait()

    means_ref[...] = got_means[...]
    pair = got[SWEEPS - 1, 2:3, 256:384]
    own_zp = jnp.where(band % 2 == 0, pair, pltpu.roll(pair, OWN, 1))
    out_ref[...] = jnp.zeros((8, 128), F32)
    out_ref[0:1, :] = own_zp

    @pl.when(is_home)
    def _():
        for slot in range(BANDS):

            @pl.when(jnp.logical_not(owns(slot)))
            def _():
                for n in range(SWEEPS):
                    fin_copy(n, slot).wait_send()
                mean_copy(slot).wait_send()

    everyone = pltpu.make_async_remote_copy(
        src_ref=parts.at[pl.ds(1, TILES - 1)],
        dst_ref=parts.at[pl.ds(1, TILES - 1)],
        send_sem=part_send,
        recv_sem=part_recv,
        device_id=((sky + 1) % TILES, band),
        device_id_type=MESH,
    )
    everyone.wait()
    by_tile = pltpu.roll(parts[...].reshape(TILES, 128), sky, 0)
    out_ref[1:2, :] = jnp.sum(by_tile, axis=0, keepdims=True) * (1.0 / (OBS * STARS * TILES))


def solve(color_terms, m, w, s, owner, colors, lists):
    vmem = pl.BlockSpec(memory_space=pltpu.VMEM)
    dma = pltpu.SemaphoreType.DMA
    return pl.pallas_call(
        solve_kernel,
        out_shape=(
            jax.ShapeDtypeStruct((8, 128), F32),
            jax.ShapeDtypeStruct((BLOCKS, ROWS), F32),
        ),
        in_specs=[pl.BlockSpec(memory_space=pltpu.SMEM)] + [vmem] * 6,
        out_specs=(vmem,) * 2,
        scratch_shapes=[
            pltpu.VMEM((8, 384), F32),
            pltpu.VMEM((8, 384), F32),
            pltpu.VMEM((BANDS, OBS, STARS), F32),
            pltpu.VMEM((BANDS, OBS, STARS), jnp.int32),
            pltpu.VMEM((BANDS, 8, 384), F32),
            pltpu.VMEM((8, 384), F32),
            pltpu.VMEM((BANDS, BLOCKS * LIST, ROWS), F32),
            pltpu.VMEM((2, BANDS, BLOCKS * LIST, WIDE), BF16),
            pltpu.VMEM((WIDE, WIDE), F32),
            pltpu.VMEM((3, 128, 512), BF16),
            pltpu.VMEM((2, 6, 1, 128), F32),
            pltpu.VMEM((2, 4, 6, 1, 128), F32),
            pltpu.VMEM((2, 6, 1, 128), F32),
            pltpu.VMEM((2, 4, 6, 1, 128), F32),
            pltpu.VMEM((SWEEPS, BANDS, 8, 384), F32),
            pltpu.VMEM((BANDS, BLOCKS, ROWS), F32),
            pltpu.VMEM((SWEEPS, 8, 384), F32),
            pltpu.VMEM((BLOCKS, ROWS), F32),
            pltpu.VMEM((TILES, 1, 128), F32),
            dma((2, CHUNKS)),
            dma((BANDS, 2, CHUNKS)),
            dma((2,)),
            dma((BANDS, 2)),
            dma((3,)),
            dma((2, 4)),
            dma((2, 4)),
            dma((2, 4)),
            dma((2, 4)),
            dma((SWEEPS, BANDS)),
            dma((SWEEPS,)),
            dma((BANDS,)),
            dma,
            dma,
            dma,
        ],
        compiler_params=pltpu.CompilerParams(has_side_effects=True, collective_id=0),
        name="solve",
    )(color_terms, m, w, s, owner, colors, lists)


def unpack_kernel(out_ref, means_ref, zp_ref, mags_ref, mis_ref):
    zp_ref[...] = out_ref[0:1, 0:OWN]
    mis_ref[...] = out_ref[1:2, :]
    for blk in range(BLOCKS):
        mags_ref[0:1, blk * ROWS : (blk + 1) * ROWS] = means_ref[blk : blk + 1, :]


def body(magnitudes, weights, slots, block_fields, owner, colors, color_terms):
    lists = jnp.concatenate(
        [block_fields.reshape(2, 128), jnp.tile(block_fields, (1, BANDS))], axis=0
    )
    out, means = solve(
        color_terms, magnitudes[0], weights[0], slots[0],
        owner.reshape(-1, 128), colors.reshape(-1, 128), lists,
    )
    vmem = pl.BlockSpec(memory_space=pltpu.VMEM)
    zp, mags, misfit = pl.pallas_call(
        unpack_kernel,
        out_shape=(
            jax.ShapeDtypeStruct((1, OWN), F32),
            jax.ShapeDtypeStruct((1, STARS), F32),
            jax.ShapeDtypeStruct((1, 128), F32),
        ),
        in_specs=[vmem] * 2,
        out_specs=(vmem,) * 3,
        name="unpack",
    )(out, means)
    return zp, mags, misfit[:, :SWEEPS].reshape(SWEEPS, 1)


def solution(mesh):
    in_specs = (
        P("band", None, "sky"),
        P("band", None, "sky"),
        P("band", None, "sky"),
        P("sky", None),
        P(),
        P(),
        P(),
    )
    out_specs = (P("band", "sky"), P("band", "sky"), P(None, "band"))
    return jax.shard_map(body, mesh=mesh, in_specs=in_specs, out_specs=out_specs, check_vma=False)
```

time: 717 us -> 118 us (0.16)
  the two profiles are of different devices: /device:TPU:2 before, /device:TPU:1 now
where the time goes in v2:
time: 118 us; the launch traced here: 117 us
  Pallas kernels  114 us (97%)
  local copies, waits for them, and re-layouts  2.01 us (2%)
    pallas_call x1, Pallas kernels, solve(): pl.pallas_call(solve_kernel, out_shape=(jax.ShapeDtypeStruct((8, 128), F3...  113 us

profile of v2, /device:TPU:1, one launch (start us, length us, event | category | flops | bytes accessed | tf_op | source)
XLA Modules:
  0.0 117.3 jit_solution(1726179440201720692)
XLA Ops:
  0.6 0.0 copy-start
  0.6 0.7 copy-done
  1.3 0.1 reshape.24
  1.4 0.1 tile.10
  1.5 0.6 pad_add_fusion.lst_ref
  2.1 112.7 %solve.1 = (f32[8,128]{1,0:T(8,128)}, f32[8,256]{1,0:T(8,128)}) custom-call(f32[4,4]{1,0:T(4,128)} %ct_ref.1, f32[8,2048]{1,0:T(8,128)} %bitcast.7, f32[8,2048]{1,0:T(8,128)} %bitcast.8, s32[8,2048]{1,0:T(8,128)} %bitcast.9, s32[32,128]{1,0:T(8,128)} %bitcast.10, s32[32,128]{1,0:T(8,128)} %bitcast.11, s32[10,128]{1,0:T(8,128)} %pad_add_fusion.lst_ref), custom_call_target="tpu_custom_call" | custom-call | tf_op jit(solution)/shard_map/solve/pallas_call | solution.py:629
  114.8 1.3 %unpack.1 = (f32[1,64]{1,0:T(1,128)}, f32[1,2048]{1,0:T(1,128)}, f32[1,128]{1,0:T(1,128)}) custom-call(f32[8,128]{1,0:T(8,128)} %get-tuple-element.8.out_ref, f32[8,256]{1,0:T(8,128)} %get-tuple-element.9.means_ref), custom_call_target="tpu_custom_call" | custom-call | tf_op jit(solution)/shard_map/unpack/pallas_call | solution.py:694
  116.1 0.0 copy-start.1
  116.1 0.7 copy-done.1
  116.7 0.5 slice_bitcast_fusion
  (1 shorter events, 0.0 us)
Async XLA Ops:
  0.6 0.7 copy-start
  116.1 0.7 copy-start.1

commit v3 on v2

--- a/solution.py
+++ b/solution.py
@@ -25,6 +25,8 @@
 SPAN = PER * ROWS
 WIDE = BANDS * NEAR
 STEPS = COLORS * SWEEPS
+PLANE = [(i, j) for i in (2, 1, 3, 0) for j in (2, 1, 3, 0)][:-1]
+LINE = [(k, c) for k in (4, 3, 5, 2, 6, 1, 7, 0) for c in (0, 1)][:-1]
 MESH = pl.DeviceIdType.MESH
 HIGH = lax.Precision.HIGHEST
 F32 = jnp.float32
@@ -106,8 +108,11 @@
             near_ref[2 * tr : 2 * tr + 1, at : at + 128] = row
             near_ref[2 * tr + 1 : 2 * tr + 2, at : at + 128] = row
     near_ref[6:8, 128:256] = jnp.zeros((2, 128), F32)
-    near_ref[6:8, 0:128] = lst_ref[0:2, 0:128].astype(F32)
-    near_ref[:, 256:384] = lst_ref[2:10, 0:128].astype(F32)
+    listed = lst_ref[...].astype(F32)
+    near_ref[:, 256:384] = jnp.concatenate([listed] * BANDS, axis=1)
+    for h in range(2):
+        row = [listed[i : i + 1] for i in range(4 * h, 4 * h + 4)]
+        near_ref[6 + h : 7 + h, 0:128] = jnp.concatenate(row, axis=1)
 
 
 def star_tables(m_ref, w_ref, s_ref, aux_ref):
@@ -129,13 +134,14 @@
 
 
 def solve_kernel(
-    ct_ref, m_ref, w_ref, s_ref, own_ref, col_ref, lst_ref,
-    out_ref, means_ref,
-    aux, near, bw, bs, ba, bn, u_ref, r_ref, mt_ref, pick2_ref,
-    first_out, first_in, out_buf, in_buf, fin, fin_means, got, got_means, parts,
-    ship_send, ship_recv, tab_send, tab_recv, local,
+    ct_ref, m_hbm, w_hbm, s_hbm, own_ref, col_ref, lst_ref,
+    out_ref,
+    m_ref, w_ref, s_ref,
+    aux, near, bm, bw, bs, ba, bn, u_ref, r_ref, mt_ref, pick2_ref,
+    first_out, first_in, out_buf, in_buf, fin, got, row_buf, plane, line,
+    load_sem, ship_send, ship_recv, mag_send, mag_recv, tab_send, tab_recv, local,
     first_send, first_recv, send, recv,
-    fin_send, fin_recv, mean_send, mean_recv, part_send, part_recv,
+    fin_send, fin_recv, plane_send, plane_recv, line_send, line_recv, go,
 ):
     sky = lax.axis_index("sky")
     band = lax.axis_index("band")
@@ -164,8 +170,16 @@
             def _():
                 pl.semaphore_signal(barrier, inc=1, device_id=(tile, slot), device_id_type=MESH)
 
+    loads = [
+        pltpu.make_async_copy(src, dst, load_sem.at[i])
+        for i, (src, dst) in enumerate(((m_hbm, m_ref), (w_hbm, w_ref), (s_hbm, s_ref)))
+    ]
+    for load in loads:
+        load.start()
+    tile_tables(sky, own_ref, col_ref, lst_ref, near)
+    for load in loads:
+        load.wait()
     star_tables(m_ref, w_ref, s_ref, aux)
-    tile_tables(sky, own_ref, col_ref, lst_ref, near)
 
     @pl.when(is_home & moves)
     def _():
@@ -194,6 +208,16 @@
             device_id_type=MESH,
         )
 
+    def mag_copy(slot):
+        return pltpu.make_async_remote_copy(
+            src_ref=m_ref,
+            dst_ref=bm.at[slot],
+            send_sem=mag_send,
+            recv_sem=mag_recv.at[slot],
+            device_id=(home_sky, home_band),
+            device_id_type=MESH,
+        )
+
     def table_copy(i, slot):
         src, dst = ((aux, ba.at[slot]), (near, bn))[i]
         return pltpu.make_async_remote_copy(
@@ -224,6 +248,7 @@
             pltpu.make_async_copy(aux, ba.at[band], local.at[0]),
             pltpu.make_async_copy(w_ref, bw.at[band], local.at[1]),
             pltpu.make_async_copy(s_ref, bs.at[band], local.at[2]),
+            pltpu.make_async_copy(m_ref, bm.at[band], local.at[3]),
         ]
         for copy in copies:
             copy.start()
@@ -268,6 +293,13 @@
         for blk in range(BLOCKS):
             if blk % PER == 0:
                 await_chunk(blk // PER)
+            if blk == BLOCKS - PER:
+                for slot in range(BANDS):
+
+                    @pl.when(jnp.logical_not(owns(slot)))
+                    def _():
+                        pl.semaphore_signal(go, inc=1, device_id=(tile, slot), device_id_type=MESH)
+
             cols = slice(blk * ROWS, (blk + 1) * ROWS)
             wide, scaled = [], []
             mean0 = [ba[b, blk : blk + 1, 0:ROWS] for b in range(BANDS)]
@@ -394,62 +426,96 @@
     outer, inner = (0, 1, 4, 5), (2, 3)
 
     def evaluate(n, z, last):
-        zb = [[None, None] for _ in range(BANDS)]
         total = jnp.zeros((8, 512), F32)
         for tr in range(3):
             pair = jnp.concatenate([z[2 * tr], z[2 * tr + 1]], axis=0)
             lhs = jnp.concatenate(split(pair, 3) + [jnp.zeros((2, 128), BF16)], axis=0)
             total = total + jnp.dot(lhs, pick2_ref[tr], preferred_element_type=F32)
         total = total[0:2] + total[2:4] + total[4:6]
-        means = []
+        means, tables = [], []
         for b in range(BANDS):
             rows = []
+            tables.append([])
             for h in range(2):
                 at = (b % 2) * 256 + h * 128
                 row = total[b // 2 : b // 2 + 1, at : at + 128]
-                fin[n, b, h : h + 1, 256:384] = row
+                tables[b].append(jnp.broadcast_to(row, (8, 128)))
                 col = columns(row)
                 for i in range(4):
                     blk = h * 4 + i
                     value = u_ref[b, blk * LIST : (blk + 1) * LIST, :] * col[i * LIST : (i + 1) * LIST, :]
                     rows.append(jnp.sum(value, axis=0, keepdims=True))
             means.append(ba[b, :, 0:ROWS] - jnp.concatenate(rows, axis=0))
-            fin[n, b, 2:3, 256:384] = z[2 + b // 2]
-            fin[n, b, 3:8, 256:384] = jnp.zeros((5, 128), F32)
+        if last:
+            for b in range(BANDS):
+                fin[b, :, 0:ROWS] = means[b]
+                fin[b, 0:1, 256:384] = z[2 + b // 2]
+                fin[b, 1:8, 256:384] = jnp.zeros((7, 128), F32)
+            for slot in range(BANDS):
+
+                @pl.when(jnp.logical_not(owns(slot)))
+                def _():
+                    fin_copy(slot).start()
+
+        lane = iota((1, 128), 1)
+        found = jnp.zeros((1, 128), F32)
         for b in range(BANDS):
             pred = mix[b][0] * means[0]
             for b2 in range(1, BANDS):
                 pred = pred + mix[b][b2] * means[b2]
-            fin[n, b, :, 0:ROWS] = pred
-            if last:
-                fin_means[b] = means[b]
-        for slot in range(BANDS):
-
-            @pl.when(jnp.logical_not(owns(slot)))
-            def _():
-                fin_copy(n, slot).start()
-                if last:
-                    mean_copy(slot).start()
-
-    def fin_copy(n, slot):
+            acc = jnp.zeros((8, 128), F32)
+            for blk in range(BLOCKS):
+                for half in range(2):
+                    at = blk * ROWS + half * 128
+                    idx = bs[b, :, at : at + 128] + (blk % 4) * LIST
+                    picked = jnp.take_along_axis(tables[b][blk // 4], idx, axis=1)
+                    left = bm[b, :, at : at + 128] - pred[blk : blk + 1, half * 128 : half * 128 + 128]
+                    left = left - picked
+                    acc = acc + bw[b, :, at : at + 128] * left * left
+            value = jnp.sum(jnp.sum(acc, axis=0, keepdims=True), axis=1, keepdims=True)
+            found = jnp.where(lane == n + b * SWEEPS, value, found)
+        row_buf[0] = row_buf[0] + found
+
+    def fin_copy(slot):
         return pltpu.make_async_remote_copy(
-            src_ref=fin.at[n, slot],
-            dst_ref=got.at[n],
-            send_sem=fin_send.at[n, slot],
-            recv_sem=fin_recv.at[n],
+            src_ref=fin.at[slot],
+            dst_ref=got,
+            send_sem=fin_send.at[slot],
+            recv_sem=fin_recv,
             device_id=(tile, slot),
             device_id_type=MESH,
         )
 
-    def mean_copy(slot):
+    x = (sky // 32) * 2 + band // 2
+    y = (sky // 8) % 4
+    z_at = sky % 8
+
+    def core_at(dx, dy, dz, core):
+        x_to, y_to, z_to = (x + dx) % 4, (y + dy) % 4, (z_at + dz) % 8
+        return (x_to // 2) * 32 + y_to * 8 + z_to, (x_to % 2) * 2 + core
+
+    def plane_copy(i):
         return pltpu.make_async_remote_copy(
-            src_ref=fin_means.at[slot],
-            dst_ref=got_means,
-            send_sem=mean_send.at[slot],
-            recv_sem=mean_recv,
-            device_id=(tile, slot),
+            src_ref=row_buf.at[0],
+            dst_ref=plane.at[x * 4 + y],
+            send_sem=plane_send.at[i],
+            recv_sem=plane_recv,
+            device_id=core_at(PLANE[i][0], PLANE[i][1], 0, 1),
             device_id_type=MESH,
         )
+
+    def line_copy(i):
+        return pltpu.make_async_remote_copy(
+            src_ref=row_buf.at[1],
+            dst_ref=line.at[z_at % 4],
+            send_sem=line_send.at[i],
+            recv_sem=line_recv,
+            device_id=core_at(0, 0, LINE[i][0], LINE[i][1]),
+            device_id_type=MESH,
+        )
+
+    def whole(ref, sem):
+        return pltpu.make_async_copy(ref, ref, sem)
 
     @pl.when(is_home)
     def _():
@@ -473,6 +539,7 @@
             out_buf[1, q] = jnp.sum(accs[q], axis=0, keepdims=True)
         for slot in (2, 3, 0, 1):
             step_copy(slot, 1).start()
+        row_buf[0] = zero
 
         def renew(q, color, pulled, old):
             return jnp.where(colors[q] == color, (known[q] + pulled) * scale[q], old)
@@ -502,8 +569,21 @@
         def step(s, z):
             p = s % 2
 
+            @pl.when((s == 2) & moves)
+            def _():
+                pl.semaphore_wait(go, 1)
+                mag_copy(band).start()
+
             @pl.when(s % COLORS == 0)
             def _():
+                @pl.when(s == COLORS)
+                def _():
+                    for slot in range(BANDS):
+
+                        @pl.when(jnp.logical_not(owns(slot)))
+                        def _():
+                            mag_copy(slot).wait_recv()
+
                 evaluate(s // COLORS - 1, z, False)
 
             z, accs = absorb(s, z, True)
@@ -525,8 +605,25 @@
         z = lax.fori_loop(1, STEPS - 1, step, tuple(z))
         z, _ = absorb(STEPS - 1, z, False)
         evaluate(SWEEPS - 1, z, True)
+        for i in range(len(PLANE)):
+            plane_copy(i).start()
+        mine = pltpu.make_async_copy(row_buf.at[0], plane.at[x * 4 + y], plane_recv)
+        mine.start()
+        whole(plane, plane_recv).wait()
+        row_buf[1] = jnp.sum(plane[...].reshape(16, 128), axis=0, keepdims=True)
+        for i in range(len(LINE)):
+            line_copy(i).start()
+        mine = pltpu.make_async_copy(row_buf.at[1], line.at[z_at % 4], line_recv)
+        mine.start()
+        for i in range(len(PLANE)):
+            plane_copy(i).wait_send()
         for slot in range(4):
             step_copy(slot, (STEPS - 1) % 2).wait_send()
+
+    @pl.when(jnp.logical_not(is_home))
+    def _():
+        pl.semaphore_wait(go, 1)
+        mag_copy(band).start()
 
     @pl.when(moves)
     def _():
@@ -538,67 +635,24 @@
         for c in range(CHUNKS):
             for i in range(2):
                 ship_copy(i, band, c).wait_send()
-
-    def squares(n):
-        @pl.when(moves)
-        def _():
-            fin_copy(n, 0).wait_recv()
-
-        @pl.when(stays)
-        def _():
-            mine = pltpu.make_async_copy(fin.at[n, band], got.at[n], local.at[0])
-            mine.start()
-            mine.wait()
-
-        acc = jnp.zeros((8, 128), F32)
-        for blk in range(BLOCKS):
-            for half in range(2):
-                at = blk * ROWS + half * 128
-                table = jnp.broadcast_to(got[n, blk // 4 : blk // 4 + 1, 256:384], (8, 128))
-                idx = s_ref[:, at : at + 128] + (blk % 4) * LIST
-                picked = jnp.take_along_axis(table, idx, axis=1)
-                left = m_ref[:, at : at + 128] - got[n, blk : blk + 1, half * 128 : half * 128 + 128]
-                left = left - picked
-                acc = acc + w_ref[:, at : at + 128] * left * left
-        total = jnp.sum(jnp.sum(acc, axis=0, keepdims=True), axis=1, keepdims=True)
-        return jnp.where(iota((1, 128), 1) == n, total, 0.0)
-
-    row = squares(0)
-    for n in range(1, SWEEPS):
-        row = row + squares(n)
-    parts[0] = row
-
-    def part(d):
-        return pltpu.make_async_remote_copy(
-            src_ref=parts.at[0],
-            dst_ref=parts.at[d],
-            send_sem=part_send,
-            recv_sem=part_recv,
-            device_id=((sky + TILES - d) % TILES, band),
-            device_id_type=MESH,
-        )
-
-    def push(d, carry):
-        part(d).start()
-        return carry
-
-    lax.fori_loop(1, TILES, push, 0)
-
-    @pl.when(moves)
-    def _():
-        mean_copy(0).wait_recv()
+        mag_copy(band).wait_send()
+        fin_copy(0).wait_recv()
 
     @pl.when(stays)
     def _():
-        mine = pltpu.make_async_copy(fin_means.at[band], got_means, local.at[1])
+        mine = pltpu.make_async_copy(fin.at[band], got, local.at[0])
         mine.start()
         mine.wait()
 
-    means_ref[...] = got_means[...]
-    pair = got[SWEEPS - 1, 2:3, 256:384]
-    own_zp = jnp.where(band % 2 == 0, pair, pltpu.roll(pair, OWN, 1))
-    out_ref[...] = jnp.zeros((8, 128), F32)
-    out_ref[0:1, :] = own_zp
+    out_ref[:, 0:256] = got[:, 0:256]
+    pair = got[0:1, 256:384]
+    out_ref[:, 256:512] = jnp.zeros((8, 256), F32)
+    out_ref[0:1, 256:384] = jnp.where(band % 2 == 0, pair, pltpu.roll(pair, OWN, 1))
+
+    whole(line, line_recv).wait()
+    total = jnp.sum(line[...].reshape(4, 128), axis=0, keepdims=True)
+    total = pltpu.roll(total, (128 - band * SWEEPS) % 128, 1)
+    out_ref[0:1, 384:512] = total * (1.0 / (OBS * STARS * TILES))
 
     @pl.when(is_home)
     def _():
@@ -606,37 +660,28 @@
 
             @pl.when(jnp.logical_not(owns(slot)))
             def _():
-                for n in range(SWEEPS):
-                    fin_copy(n, slot).wait_send()
-                mean_copy(slot).wait_send()
-
-    everyone = pltpu.make_async_remote_copy(
-        src_ref=parts.at[pl.ds(1, TILES - 1)],
-        dst_ref=parts.at[pl.ds(1, TILES - 1)],
-        send_sem=part_send,
-        recv_sem=part_recv,
-        device_id=((sky + 1) % TILES, band),
-        device_id_type=MESH,
-    )
-    everyone.wait()
-    by_tile = pltpu.roll(parts[...].reshape(TILES, 128), sky, 0)
-    out_ref[1:2, :] = jnp.sum(by_tile, axis=0, keepdims=True) * (1.0 / (OBS * STARS * TILES))
+                fin_copy(slot).wait_send()
+
+        for i in range(len(LINE)):
+            line_copy(i).wait_send()
 
 
 def solve(color_terms, m, w, s, owner, colors, lists):
     vmem = pl.BlockSpec(memory_space=pltpu.VMEM)
+    hbm = pl.BlockSpec(memory_space=pl.ANY)
     dma = pltpu.SemaphoreType.DMA
     return pl.pallas_call(
         solve_kernel,
-        out_shape=(
-            jax.ShapeDtypeStruct((8, 128), F32),
-            jax.ShapeDtypeStruct((BLOCKS, ROWS), F32),
-        ),
-        in_specs=[pl.BlockSpec(memory_space=pltpu.SMEM)] + [vmem] * 6,
-        out_specs=(vmem,) * 2,
+        out_shape=jax.ShapeDtypeStruct((8, 512), F32),
+        in_specs=[pl.BlockSpec(memory_space=pltpu.SMEM)] + [hbm] * 3 + [vmem] * 3,
+        out_specs=vmem,
         scratch_shapes=[
+            pltpu.VMEM((OBS, STARS), F32),
+            pltpu.VMEM((OBS, STARS), F32),
+            pltpu.VMEM((OBS, STARS), jnp.int32),
             pltpu.VMEM((8, 384), F32),
             pltpu.VMEM((8, 384), F32),
+            pltpu.VMEM((BANDS, OBS, STARS), F32),
             pltpu.VMEM((BANDS, OBS, STARS), F32),
             pltpu.VMEM((BANDS, OBS, STARS), jnp.int32),
             pltpu.VMEM((BANDS, 8, 384), F32),
@@ -649,46 +694,47 @@
             pltpu.VMEM((2, 4, 6, 1, 128), F32),
             pltpu.VMEM((2, 6, 1, 128), F32),
             pltpu.VMEM((2, 4, 6, 1, 128), F32),
-            pltpu.VMEM((SWEEPS, BANDS, 8, 384), F32),
-            pltpu.VMEM((BANDS, BLOCKS, ROWS), F32),
-            pltpu.VMEM((SWEEPS, 8, 384), F32),
-            pltpu.VMEM((BLOCKS, ROWS), F32),
-            pltpu.VMEM((TILES, 1, 128), F32),
+            pltpu.VMEM((BANDS, 8, 384), F32),
+            pltpu.VMEM((8, 384), F32),
+            pltpu.VMEM((2, 1, 128), F32),
+            pltpu.VMEM((16, 1, 128), F32),
+            pltpu.VMEM((4, 1, 128), F32),
+            dma((3,)),
             dma((2, CHUNKS)),
             dma((BANDS, 2, CHUNKS)),
+            dma,
+            dma((BANDS,)),
             dma((2,)),
             dma((BANDS, 2)),
-            dma((3,)),
+            dma((4,)),
             dma((2, 4)),
             dma((2, 4)),
             dma((2, 4)),
             dma((2, 4)),
-            dma((SWEEPS, BANDS)),
-            dma((SWEEPS,)),
             dma((BANDS,)),
             dma,
+            dma((len(PLANE),)),
             dma,
+            dma((len(LINE),)),
             dma,
+            pltpu.SemaphoreType.REGULAR,
         ],
         compiler_params=pltpu.CompilerParams(has_side_effects=True, collective_id=0),
         name="solve",
     )(color_terms, m, w, s, owner, colors, lists)
 
 
-def unpack_kernel(out_ref, means_ref, zp_ref, mags_ref, mis_ref):
-    zp_ref[...] = out_ref[0:1, 0:OWN]
-    mis_ref[...] = out_ref[1:2, :]
+def unpack_kernel(out_ref, zp_ref, mags_ref, mis_ref):
+    zp_ref[...] = out_ref[0:1, 256 : 256 + OWN]
+    mis_ref[...] = out_ref[0:1, 384 : 384 + SWEEPS]
     for blk in range(BLOCKS):
-        mags_ref[0:1, blk * ROWS : (blk + 1) * ROWS] = means_ref[blk : blk + 1, :]
+        mags_ref[0:1, blk * ROWS : (blk + 1) * ROWS] = out_ref[blk : blk + 1, 0:ROWS]
 
 
 def body(magnitudes, weights, slots, block_fields, owner, colors, color_terms):
-    lists = jnp.concatenate(
-        [block_fields.reshape(2, 128), jnp.tile(block_fields, (1, BANDS))], axis=0
-    )
-    out, means = solve(
+    out = solve(
         color_terms, magnitudes[0], weights[0], slots[0],
-        owner.reshape(-1, 128), colors.reshape(-1, 128), lists,
+        owner.reshape(-1, 128), colors.reshape(-1, 128), block_fields,
     )
     vmem = pl.BlockSpec(memory_space=pltpu.VMEM)
     zp, mags, misfit = pl.pallas_call(
@@ -696,13 +742,13 @@
         out_shape=(
             jax.ShapeDtypeStruct((1, OWN), F32),
             jax.ShapeDtypeStruct((1, STARS), F32),
-            jax.ShapeDtypeStruct((1, 128), F32),
+            jax.ShapeDtypeStruct((1, SWEEPS), F32),
         ),
-        in_specs=[vmem] * 2,
+        in_specs=[vmem],
         out_specs=(vmem,) * 3,
         name="unpack",
-    )(out, means)
-    return zp, mags, misfit[:, :SWEEPS].reshape(SWEEPS, 1)
+    )(out)
+    return zp, mags, misfit.T
 
 
 def solution(mesh):

time: 118 us -> 110 us (0.932)
  Pallas kernels: 114 us -> 109 us
  local copies, waits for them, and re-layouts: 2.01 us -> 0 us
    pallas_call x1, Pallas kernels: 113 us -> 108 us  [solve(): pl.pallas_call(solve_kernel, out_shape=jax.ShapeDtypeStruct((8, 512), F32...]
    unnamed x4 -> x0, local copies, waits for them, and re-layouts: 1.33 us -> none
where the time goes in v3:
time: 110 us
  Pallas kernels  109 us (99%)
    pallas_call x1, Pallas kernels, solve(): pl.pallas_call(solve_kernel, out_shape=jax.ShapeDtypeStruct((8, 512), F32...  108 us

profile of v3, /device:TPU:1, one launch (start us, length us, event | category | flops | bytes accessed | tf_op | source)
XLA Modules:
  0.0 109.8 jit_solution(8662733914649928431)
XLA Ops:
  0.6 107.9 %solve.1.out_ref = f32[8,512]{1,0:T(8,128)} custom-call(f32[4,4]{1,0:T(4,128)} %ct_ref.1, f32[8,2048]{1,0:T(8,128)} %bitcast.6, f32[8,2048]{1,0:T(8,128)} %bitcast.7, s32[8,2048]{1,0:T(8,128)} %bitcast.8, s32[32,128]{1,0:T(8,128)} %bitcast.9, s32[32,128]{1,0:T(8,128)} %bitcast.10, s32[8,32]{1,0:T(8,128)} %lst_ref.1), custom_call_target="tpu_custom_call" | custom-call | tf_op jit(solution)/shard_map/solve/pallas_call | solution.py:673
  108.5 1.3 %unpack.1 = (f32[1,64]{1,0:T(1,128)}, f32[1,2048]{1,0:T(1,128)}, f32[1,4]{1,0:T(1,128)}) custom-call(f32[8,512]{1,0:T(8,128)} %solve.1.out_ref), custom_call_target="tpu_custom_call" | custom-call | tf_op jit(solution)/shard_map/unpack/pallas_call | solution.py:740

commit v4 on v3

--- a/solution.py
+++ b/solution.py
@@ -20,9 +20,9 @@
 LIST = 32
 OWN = 64
 NEAR = 3 * OWN
-CHUNKS = 4
-PER = BLOCKS // CHUNKS
-SPAN = PER * ROWS
+CUTS = (0, 2, 4, 6, 7, 8)
+CHUNKS = len(CUTS) - 1
+EARLY = 2
 WIDE = BANDS * NEAR
 STEPS = COLORS * SWEEPS
 PLANE = [(i, j) for i in (2, 1, 3, 0) for j in (2, 1, 3, 0)][:-1]
@@ -115,31 +115,38 @@
         near_ref[6 + h : 7 + h, 0:128] = jnp.concatenate(row, axis=1)
 
 
-def star_tables(m_ref, w_ref, s_ref, aux_ref):
+def star_means(m_ref, w_ref, mean_ref):
+    for blk in range(BLOCKS):
+        cols = slice(blk * ROWS, (blk + 1) * ROWS)
+        top = jnp.sum(w_ref[:, cols] * m_ref[:, cols], axis=0, keepdims=True)
+        mean_ref[blk : blk + 1, :] = top / jnp.sum(w_ref[:, cols], axis=0, keepdims=True)
+
+
+def list_sums(m_ref, w_ref, s_ref, pred, aux_ref):
     entries = iota((LIST, ROWS), 0)
-    sums = [jnp.zeros((1, 128), F32) for _ in range(2)]
+    rows = [jnp.zeros((1, 128), F32) for _ in range(4)]
     for blk in range(BLOCKS):
         cols = slice(blk * ROWS, (blk + 1) * ROWS)
         acc = jnp.zeros((LIST, ROWS), F32)
+        wts = jnp.zeros((LIST, ROWS), F32)
         for k in range(OBS):
-            value = w_ref[k : k + 1, cols] * m_ref[k : k + 1, cols]
-            acc = acc + jnp.where(s_ref[k : k + 1, cols] == entries, value, 0.0)
-        top = jnp.sum(w_ref[:, cols] * m_ref[:, cols], axis=0, keepdims=True)
-        aux_ref[blk : blk + 1, 0:ROWS] = top / jnp.sum(w_ref[:, cols], axis=0, keepdims=True)
-        col = jnp.sum(acc, axis=1, keepdims=True)
-        sums[blk // 4] = sums[blk // 4] + as_row(col, (blk % 4) * LIST)
-    aux_ref[2:8, 256:384] = jnp.zeros((6, 128), F32)
-    for h in range(2):
-        aux_ref[h : h + 1, 256:384] = sums[h]
+            hit = s_ref[k : k + 1, cols] == entries
+            wk = w_ref[k : k + 1, cols]
+            wts = wts + jnp.where(hit, wk, 0.0)
+            acc = acc + jnp.where(hit, wk * (m_ref[k : k + 1, cols] - pred[blk : blk + 1]), 0.0)
+        h, at = blk // 4, (blk % 4) * LIST
+        rows[h] = rows[h] + as_row(jnp.sum(acc, axis=1, keepdims=True), at)
+        rows[2 + h] = rows[2 + h] + as_row(jnp.sum(wts, axis=1, keepdims=True), at)
+    aux_ref[...] = jnp.concatenate(rows + [jnp.zeros((4, 128), F32)], axis=0)
 
 
 def solve_kernel(
     ct_ref, m_hbm, w_hbm, s_hbm, own_ref, col_ref, lst_ref,
     out_ref,
     m_ref, w_ref, s_ref,
-    aux, near, bm, bw, bs, ba, bn, u_ref, r_ref, mt_ref, pick2_ref,
+    mean, mates, aux, near, bm, bw, bs, ba, bt, bn, u_ref, r_ref, mt_ref, pick2_ref,
     first_out, first_in, out_buf, in_buf, fin, got, row_buf, plane, line,
-    load_sem, ship_send, ship_recv, mag_send, mag_recv, tab_send, tab_recv, local,
+    load_sem, mate_send, mate_recv, ship_send, ship_recv, mag_send, mag_recv, tab_send, tab_recv, local,
     first_send, first_recv, send, recv,
     fin_send, fin_recv, plane_send, plane_recv, line_send, line_recv, go,
 ):
@@ -155,6 +162,9 @@
         return (tile == sky) & (band == slot)
 
     barrier = pltpu.get_barrier_semaphore()
+    mates_of = [(band + i) % BANDS for i in range(1, BANDS)]
+    for mate in mates_of:
+        pl.semaphore_signal(barrier, inc=1, device_id=(sky, mate), device_id_type=MESH)
 
     @pl.when(moves)
     def _():
@@ -179,22 +189,22 @@
     tile_tables(sky, own_ref, col_ref, lst_ref, near)
     for load in loads:
         load.wait()
-    star_tables(m_ref, w_ref, s_ref, aux)
+    star_means(m_ref, w_ref, mean)
 
     @pl.when(is_home & moves)
     def _():
-        pl.semaphore_wait(barrier, 9)
+        pl.semaphore_wait(barrier, 12)
 
     @pl.when(is_home & stays)
     def _():
-        pl.semaphore_wait(barrier, 7)
+        pl.semaphore_wait(barrier, 10)
 
     @pl.when(jnp.logical_not(is_home))
     def _():
-        pl.semaphore_wait(barrier, 1)
+        pl.semaphore_wait(barrier, 4)
 
     def chunk(ref, slot, c):
-        at = pl.ds(c * SPAN, SPAN)
+        at = pl.ds(CUTS[c] * ROWS, (CUTS[c + 1] - CUTS[c]) * ROWS)
         return ref.at[:, at] if slot is None else ref.at[slot, :, at]
 
     def ship_copy(i, slot, c):
@@ -218,8 +228,18 @@
             device_id_type=MESH,
         )
 
+    def mate_copy(i):
+        return pltpu.make_async_remote_copy(
+            src_ref=mean,
+            dst_ref=mates.at[band],
+            send_sem=mate_send.at[i],
+            recv_sem=mate_recv.at[i],
+            device_id=(sky, mates_of[i]),
+            device_id_type=MESH,
+        )
+
     def table_copy(i, slot):
-        src, dst = ((aux, ba.at[slot]), (near, bn))[i]
+        src, dst = ((mean, ba.at[slot]), (near, bn), (aux, bt.at[slot]))[i]
         return pltpu.make_async_remote_copy(
             src_ref=src,
             dst_ref=dst,
@@ -231,6 +251,11 @@
 
     teller = 0
 
+    for i in range(BANDS - 1):
+        mate_copy(i).start()
+    keep = pltpu.make_async_copy(mean, mates.at[band], local.at[4])
+    keep.start()
+
     @pl.when(moves)
     def _():
         @pl.when(band == teller)
@@ -238,22 +263,9 @@
             table_copy(1, band).start()
 
         table_copy(0, band).start()
-        for c in range(CHUNKS):
+        for c in range(EARLY):
             for i in range(2):
                 ship_copy(i, band, c).start()
-
-    @pl.when(stays)
-    def _():
-        copies = [
-            pltpu.make_async_copy(aux, ba.at[band], local.at[0]),
-            pltpu.make_async_copy(w_ref, bw.at[band], local.at[1]),
-            pltpu.make_async_copy(s_ref, bs.at[band], local.at[2]),
-            pltpu.make_async_copy(m_ref, bm.at[band], local.at[3]),
-        ]
-        for copy in copies:
-            copy.start()
-        for copy in copies:
-            copy.wait()
 
     mix = []
     for b in range(BANDS):
@@ -262,6 +274,41 @@
             total = total + ct_ref[b, b2]
         mix.append([ct_ref[b, b2] + (1.0 - total if b == b2 else 0.0) for b2 in range(BANDS)])
 
+    keep.wait()
+    for i in range(BANDS - 1):
+        mate_copy(i).wait_recv()
+    pred = jnp.zeros((BLOCKS, ROWS), F32)
+    for b2 in range(BANDS):
+        factor = mix[0][b2]
+        for b in range(1, BANDS):
+            factor = jnp.where(band == b, mix[b][b2], factor)
+        pred = pred + factor * mates[b2]
+    list_sums(m_ref, w_ref, s_ref, pred, aux)
+
+    @pl.when(moves)
+    def _():
+        table_copy(2, band).start()
+        for c in range(EARLY, CHUNKS):
+            for i in range(2):
+                ship_copy(i, band, c).start()
+
+    @pl.when(stays)
+    def _():
+        copies = [
+            pltpu.make_async_copy(mean, ba.at[band], local.at[0]),
+            pltpu.make_async_copy(w_ref, bw.at[band], local.at[1]),
+            pltpu.make_async_copy(s_ref, bs.at[band], local.at[2]),
+            pltpu.make_async_copy(m_ref, bm.at[band], local.at[3]),
+            pltpu.make_async_copy(aux, bt.at[band], local.at[4]),
+        ]
+        for copy in copies:
+            copy.start()
+        for copy in copies:
+            copy.wait()
+
+    for i in range(BANDS - 1):
+        mate_copy(i).wait_send()
+
     def await_tables():
         table_copy(1, teller).wait_recv()
         for slot in range(BANDS):
@@ -269,6 +316,13 @@
             @pl.when(jnp.logical_not(owns(slot)))
             def _():
                 table_copy(0, slot).wait_recv()
+
+    def await_sums():
+        for slot in range(BANDS):
+
+            @pl.when(jnp.logical_not(owns(slot)))
+            def _():
+                table_copy(2, slot).wait_recv()
 
     def await_chunk(c):
         for slot in range(BANDS):
@@ -288,12 +342,23 @@
                 mixes = jnp.where((row_band == b2) & (lane_list == b), mix[b][b2], mixes)
         entries = iota((LIST, ROWS), 0)
         await_tables()
-        known = [[ba[b, h : h + 1, 256:384] for h in range(2)] for b in range(BANDS)]
-        dens = [[jnp.zeros((1, 128), F32) for _ in range(2)] for _ in range(BANDS)]
+        pick = []
+        for tr in range(3):
+            col = as_column(bn[2 * tr : 2 * tr + 1, 0:128], OWN)
+            one = jnp.concatenate(
+                [jnp.where(col == bn[6 + h : 7 + h, 0:128], 1.0, 0.0) for h in range(2)], axis=1
+            ).astype(BF16)
+            none = jnp.zeros((OWN, 256), BF16)
+            pick2_ref[tr, 0:OWN, 0:256] = one
+            pick2_ref[tr, OWN:128, 0:256] = none
+            pick2_ref[tr, 0:OWN, 256:512] = none
+            pick2_ref[tr, OWN:128, 256:512] = one
+            pick.append(one)
+        pick = jnp.concatenate(pick, axis=0)
         for blk in range(BLOCKS):
-            if blk % PER == 0:
-                await_chunk(blk // PER)
-            if blk == BLOCKS - PER:
+            if blk in CUTS:
+                await_chunk(CUTS.index(blk))
+            if blk == CUTS[-2]:
                 for slot in range(BANDS):
 
                     @pl.when(jnp.logical_not(owns(slot)))
@@ -302,7 +367,6 @@
 
             cols = slice(blk * ROWS, (blk + 1) * ROWS)
             wide, scaled = [], []
-            mean0 = [ba[b, blk : blk + 1, 0:ROWS] for b in range(BANDS)]
             for b in range(BANDS):
                 acc = jnp.zeros((LIST, ROWS), F32)
                 for k in range(OBS):
@@ -312,13 +376,6 @@
                 wide.append(acc)
                 scaled.append(acc * (1.0 / star_w))
                 u_ref[b, blk * LIST : (blk + 1) * LIST, :] = scaled[b]
-                pred0 = mix[b][0] * mean0[0]
-                for b2 in range(1, BANDS):
-                    pred0 = pred0 + mix[b][b2] * mean0[b2]
-                h, at = blk // 4, (blk % 4) * LIST
-                pulled = jnp.sum(acc * pred0, axis=1, keepdims=True)
-                known[b][h] = known[b][h] - as_row(pulled, at)
-                dens[b][h] = dens[b][h] + as_row(jnp.sum(acc, axis=1, keepdims=True), at)
             w_hi, w_lo = split(jnp.concatenate(wide, axis=0), 2)
             u_hi, u_lo = split(jnp.concatenate(scaled, axis=0), 2)
             dims = (((1,), (1,)), ((), ()))
@@ -340,21 +397,20 @@
                         r_ref[
                             i, b2, blk * LIST : (blk + 1) * LIST, q * 128 : (q + 1) * 128
                         ] = moved[at : at + LIST]
-        pick = []
-        for tr in range(3):
-            col = as_column(bn[2 * tr : 2 * tr + 1, 0:128], OWN)
-            one = jnp.concatenate(
-                [jnp.where(col == bn[6 + h : 7 + h, 0:128], 1.0, 0.0) for h in range(2)], axis=1
-            ).astype(BF16)
-            none = jnp.zeros((OWN, 256), BF16)
-            pick2_ref[tr, 0:OWN, 0:256] = one
-            pick2_ref[tr, OWN:128, 0:256] = none
-            pick2_ref[tr, 0:OWN, 256:512] = none
-            pick2_ref[tr, OWN:128, 256:512] = one
-            pick.append(one)
-        pick = jnp.concatenate(pick, axis=0)
-        rows = [jnp.concatenate(known[b], axis=1) for b in range(BANDS)]
-        rows += [jnp.concatenate(dens[b], axis=1) for b in range(BANDS)]
+            if blk == CUTS[EARLY] - 1:
+                await_sums()
+                first_sums(pick)
+            if blk in (3, 7):
+                at = slice((blk - 3) * LIST, (blk + 1) * LIST)
+                for b2 in range(BANDS):
+                    total = jnp.dot(pick[:, at], r_ref[0, b2, at, :], preferred_element_type=F32)
+                    total = total + jnp.dot(pick[:, at], r_ref[1, b2, at, :], preferred_element_type=F32)
+                    rows = slice(b2 * NEAR, (b2 + 1) * NEAR)
+                    mt_ref[rows, :] = total if blk == 3 else mt_ref[rows, :] + total
+
+    def first_sums(pick):
+        rows = [jnp.concatenate([bt[b, h : h + 1, :] for h in range(2)], axis=1) for b in range(BANDS)]
+        rows += [jnp.concatenate([bt[b, h : h + 1, :] for h in (2, 3)], axis=1) for b in range(BANDS)]
         terms = jnp.concatenate(split(jnp.concatenate(rows, axis=0), 3), axis=0)
         sums = lax.dot_general(terms, pick, (((1,), (1,)), ((), ())), preferred_element_type=F32)
         sums = sums[0:8] + sums[8:16] + sums[16:24]
@@ -367,13 +423,8 @@
                     [sums[low : low + 1, at], sums[high : high + 1, at]], axis=1
                 )
         for i in range(2):
-            for slot in range(4):
+            for slot in (2, 3, 0, 1):
                 first_copy(slot, i).start()
-        for b2 in range(BANDS):
-            total = jnp.dot(pick, r_ref[0, b2], preferred_element_type=F32)
-            total = total + jnp.dot(pick, r_ref[1, b2], preferred_element_type=F32)
-            mt_ref[b2 * NEAR : (b2 + 1) * NEAR, :] = total
-
     def first_copy(slot, i):
         return pltpu.make_async_remote_copy(
             src_ref=first_out.at[i],
@@ -445,7 +496,7 @@
                     blk = h * 4 + i
                     value = u_ref[b, blk * LIST : (blk + 1) * LIST, :] * col[i * LIST : (i + 1) * LIST, :]
                     rows.append(jnp.sum(value, axis=0, keepdims=True))
-            means.append(ba[b, :, 0:ROWS] - jnp.concatenate(rows, axis=0))
+            means.append(ba[b] - jnp.concatenate(rows, axis=0))
         if last:
             for b in range(BANDS):
                 fin[b, :, 0:ROWS] = means[b]
@@ -632,6 +683,7 @@
             table_copy(1, band).wait_send()
 
         table_copy(0, band).wait_send()
+        table_copy(2, band).wait_send()
         for c in range(CHUNKS):
             for i in range(2):
                 ship_copy(i, band, c).wait_send()
@@ -679,12 +731,15 @@
             pltpu.VMEM((OBS, STARS), F32),
             pltpu.VMEM((OBS, STARS), F32),
             pltpu.VMEM((OBS, STARS), jnp.int32),
-            pltpu.VMEM((8, 384), F32),
+            pltpu.VMEM((BLOCKS, ROWS), F32),
+            pltpu.VMEM((BANDS, BLOCKS, ROWS), F32),
+            pltpu.VMEM((8, 128), F32),
             pltpu.VMEM((8, 384), F32),
             pltpu.VMEM((BANDS, OBS, STARS), F32),
             pltpu.VMEM((BANDS, OBS, STARS), F32),
             pltpu.VMEM((BANDS, OBS, STARS), jnp.int32),
-            pltpu.VMEM((BANDS, 8, 384), F32),
+            pltpu.VMEM((BANDS, BLOCKS, ROWS), F32),
+            pltpu.VMEM((BANDS, 8, 128), F32),
             pltpu.VMEM((8, 384), F32),
             pltpu.VMEM((BANDS, BLOCKS * LIST, ROWS), F32),
             pltpu.VMEM((2, BANDS, BLOCKS * LIST, WIDE), BF16),
@@ -700,13 +755,15 @@
             pltpu.VMEM((16, 1, 128), F32),
             pltpu.VMEM((4, 1, 128), F32),
             dma((3,)),
+            dma((BANDS - 1,)),
+            dma((BANDS - 1,)),
             dma((2, CHUNKS)),
             dma((BANDS, 2, CHUNKS)),
             dma,
             dma((BANDS,)),
-            dma((2,)),
-            dma((BANDS, 2)),
-            dma((4,)),
+            dma((3,)),
+            dma((BANDS, 3)),
+            dma((5,)),
             dma((2, 4)),
             dma((2, 4)),
             dma((2, 4)),

time: 110 us -> 108 us (0.982)
  Pallas kernels: 109 us -> 107 us
    pallas_call x1, Pallas kernels: 108 us -> 106 us  [solve(): pl.pallas_call(solve_kernel, out_shape=jax.ShapeDtypeStruct((8, 512), F32...]
where the time goes in v4:
time: 108 us
  Pallas kernels  107 us (99%)
    pallas_call x1, Pallas kernels, solve(): pl.pallas_call(solve_kernel, out_shape=jax.ShapeDtypeStruct((8, 512), F32...  106 us

profile of v4, /device:TPU:1, one launch (start us, length us, event | category | flops | bytes accessed | tf_op | source)
XLA Modules:
  0.0 108.0 jit_solution(6041598815306273865)
XLA Ops:
  0.6 106.1 %solve.1.out_ref = f32[8,512]{1,0:T(8,128)} custom-call(f32[4,4]{1,0:T(4,128)} %ct_ref.1, f32[8,2048]{1,0:T(8,128)} %bitcast.6, f32[8,2048]{1,0:T(8,128)} %bitcast.7, s32[8,2048]{1,0:T(8,128)} %bitcast.8, s32[32,128]{1,0:T(8,128)} %bitcast.9, s32[32,128]{1,0:T(8,128)} %bitcast.10, s32[8,32]{1,0:T(8,128)} %lst_ref.1), custom_call_target="tpu_custom_call" | custom-call | tf_op jit(solution)/shard_map/solve/pallas_call | solution.py:725
  106.7 1.3 %unpack.1 = (f32[1,64]{1,0:T(1,128)}, f32[1,2048]{1,0:T(1,128)}, f32[1,4]{1,0:T(1,128)}) custom-call(f32[8,512]{1,0:T(8,128)} %solve.1.out_ref), custom_call_target="tpu_custom_call" | custom-call | tf_op jit(solution)/shard_map/unpack/pallas_call | solution.py:797

commit v5 on v4

--- a/solution.py
+++ b/solution.py
@@ -141,9 +141,9 @@
 
 
 def solve_kernel(
-    ct_ref, m_hbm, w_hbm, s_hbm, own_ref, col_ref, lst_ref,
+    ct_hbm, m_hbm, w_hbm, s_hbm, own_hbm, col_hbm, lst_hbm,
     out_ref,
-    m_ref, w_ref, s_ref,
+    ct_ref, m_ref, w_ref, s_ref, own_ref, col_ref, lst_ref,
     mean, mates, aux, near, bm, bw, bs, ba, bt, bn, u_ref, r_ref, mt_ref, pick2_ref,
     first_out, first_in, out_buf, in_buf, fin, got, row_buf, plane, line,
     load_sem, mate_send, mate_recv, ship_send, ship_recv, mag_send, mag_recv, tab_send, tab_recv, local,
@@ -182,12 +182,19 @@
 
     loads = [
         pltpu.make_async_copy(src, dst, load_sem.at[i])
-        for i, (src, dst) in enumerate(((m_hbm, m_ref), (w_hbm, w_ref), (s_hbm, s_ref)))
+        for i, (src, dst) in enumerate(
+            (
+                (own_hbm, own_ref), (col_hbm, col_ref), (lst_hbm, lst_ref),
+                (m_hbm, m_ref), (w_hbm, w_ref), (s_hbm, s_ref), (ct_hbm, ct_ref),
+            )
+        )
     ]
     for load in loads:
         load.start()
+    for load in loads[:3]:
+        load.wait()
     tile_tables(sky, own_ref, col_ref, lst_ref, near)
-    for load in loads:
+    for load in loads[3:]:
         load.wait()
     star_means(m_ref, w_ref, mean)
 
@@ -724,13 +731,17 @@
     dma = pltpu.SemaphoreType.DMA
     return pl.pallas_call(
         solve_kernel,
-        out_shape=jax.ShapeDtypeStruct((8, 512), F32),
-        in_specs=[pl.BlockSpec(memory_space=pltpu.SMEM)] + [hbm] * 3 + [vmem] * 3,
+        out_shape=pltpu.VMEM((8, 512), F32),
+        in_specs=[hbm] * 7,
         out_specs=vmem,
         scratch_shapes=[
+            pltpu.SMEM(color_terms.shape, F32),
             pltpu.VMEM((OBS, STARS), F32),
             pltpu.VMEM((OBS, STARS), F32),
             pltpu.VMEM((OBS, STARS), jnp.int32),
+            pltpu.VMEM(owner.shape, jnp.int32),
+            pltpu.VMEM(colors.shape, jnp.int32),
+            pltpu.VMEM(lists.shape, jnp.int32),
             pltpu.VMEM((BLOCKS, ROWS), F32),
             pltpu.VMEM((BANDS, BLOCKS, ROWS), F32),
             pltpu.VMEM((8, 128), F32),
@@ -754,7 +765,7 @@
             pltpu.VMEM((2, 1, 128), F32),
             pltpu.VMEM((16, 1, 128), F32),
             pltpu.VMEM((4, 1, 128), F32),
-            dma((3,)),
+            dma((7,)),
             dma((BANDS - 1,)),
             dma((BANDS - 1,)),
             dma((2, CHUNKS)),
@@ -794,6 +805,7 @@
         owner.reshape(-1, 128), colors.reshape(-1, 128), block_fields,
     )
     vmem = pl.BlockSpec(memory_space=pltpu.VMEM)
+    out = pltpu.with_memory_space_constraint(out, pltpu.VMEM)
     zp, mags, misfit = pl.pallas_call(
         unpack_kernel,
         out_shape=(

time: 108 us -> 106 us (0.981)
  Pallas kernels: 107 us -> 105 us
    pallas_call x1, Pallas kernels: 106 us -> 104 us  [solve(): pl.pallas_call(solve_kernel, out_shape=pltpu.VMEM((8, 512), F32), in_spec...]
where the time goes in v5:
time: 106 us
  Pallas kernels  105 us (99%)
    pallas_call x1, Pallas kernels, solve(): pl.pallas_call(solve_kernel, out_shape=pltpu.VMEM((8, 512), F32), in_spec...  104 us

profile of v5, /device:TPU:1, one launch (start us, length us, event | category | flops | bytes accessed | tf_op | source)
XLA Modules:
  0.0 105.7 jit_solution(8413104721132250995)
XLA Ops:
  0.6 104.4 %solve.1.out_ref = f32[8,512]{1,0:T(8,128)S(1)} custom-call(f32[4,4]{1,0:T(4,128)} %ct_hbm.1, f32[8,2048]{1,0:T(8,128)} %bitcast.6, f32[8,2048]{1,0:T(8,128)} %bitcast.7, s32[8,2048]{1,0:T(8,128)} %bitcast.8, s32[32,128]{1,0:T(8,128)} %bitcast.9, s32[32,128]{1,0:T(8,128)} %bitcast.10, s32[8,32]{1,0:T(8,128)} %lst_hbm.1), custom_call_target="tpu_custom_call" | custom-call | tf_op jit(solution)/shard_map/solve/pallas_call | solution.py:732
  105.1 0.6 unpack.1

commit v6 on v5

--- a/solution.py
+++ b/solution.py
@@ -184,17 +184,14 @@
         pltpu.make_async_copy(src, dst, load_sem.at[i])
         for i, (src, dst) in enumerate(
             (
-                (own_hbm, own_ref), (col_hbm, col_ref), (lst_hbm, lst_ref),
-                (m_hbm, m_ref), (w_hbm, w_ref), (s_hbm, s_ref), (ct_hbm, ct_ref),
+                (w_hbm, w_ref), (s_hbm, s_ref), (m_hbm, m_ref),
+                (own_hbm, own_ref), (col_hbm, col_ref), (lst_hbm, lst_ref), (ct_hbm, ct_ref),
             )
         )
     ]
     for load in loads:
         load.start()
     for load in loads[:3]:
-        load.wait()
-    tile_tables(sky, own_ref, col_ref, lst_ref, near)
-    for load in loads[3:]:
         load.wait()
     star_means(m_ref, w_ref, mean)
 
@@ -265,12 +262,20 @@
 
     @pl.when(moves)
     def _():
+        for i in range(2):
+            ship_copy(i, band, 0).start()
+
+    for load in loads[3:]:
+        load.wait()
+    tile_tables(sky, own_ref, col_ref, lst_ref, near)
+
+    @pl.when(moves)
+    def _():
         @pl.when(band == teller)
         def _():
             table_copy(1, band).start()
 
-        table_copy(0, band).start()
-        for c in range(EARLY):
+        for c in range(1, EARLY):
             for i in range(2):
                 ship_copy(i, band, c).start()
 
@@ -298,6 +303,7 @@
         for c in range(EARLY, CHUNKS):
             for i in range(2):
                 ship_copy(i, band, c).start()
+        table_copy(0, band).start()
 
     @pl.when(stays)
     def _():
@@ -318,11 +324,6 @@
 
     def await_tables():
         table_copy(1, teller).wait_recv()
-        for slot in range(BANDS):
-
-            @pl.when(jnp.logical_not(owns(slot)))
-            def _():
-                table_copy(0, slot).wait_recv()
 
     def await_sums():
         for slot in range(BANDS):
@@ -640,6 +641,7 @@
 
                         @pl.when(jnp.logical_not(owns(slot)))
                         def _():
+                            table_copy(0, slot).wait_recv()
                             mag_copy(slot).wait_recv()
 
                 evaluate(s // COLORS - 1, z, False)

time: 106 us -> 105 us (level)
  no operation moved by 1% of the time
where the time goes in v6:
time: 105 us
  Pallas kernels  104 us (99%)
    pallas_call x1, Pallas kernels, solve(): pl.pallas_call(solve_kernel, out_shape=pltpu.VMEM((8, 512), F32), in_spec...  104 us

profile of v6, /device:TPU:1, one launch (start us, length us, event | category | flops | bytes accessed | tf_op | source)
XLA Modules:
  0.0 105.0 jit_solution(15207373300956697729)
XLA Ops:
  0.6 103.8 %solve.1.out_ref = f32[8,512]{1,0:T(8,128)S(1)} custom-call(f32[4,4]{1,0:T(4,128)} %ct_hbm.1, f32[8,2048]{1,0:T(8,128)} %bitcast.6, f32[8,2048]{1,0:T(8,128)} %bitcast.7, s32[8,2048]{1,0:T(8,128)} %bitcast.8, s32[32,128]{1,0:T(8,128)} %bitcast.9, s32[32,128]{1,0:T(8,128)} %bitcast.10, s32[8,32]{1,0:T(8,128)} %lst_hbm.1), custom_call_target="tpu_custom_call" | custom-call | tf_op jit(solution)/shard_map/solve/pallas_call | solution.py:734
  104.4 0.6 unpack.1

commit v7 on v6

--- a/solution.py
+++ b/solution.py
@@ -20,7 +20,7 @@
 LIST = 32
 OWN = 64
 NEAR = 3 * OWN
-CUTS = (0, 2, 4, 6, 7, 8)
+CUTS = (0, 2, 4, 6, 8)
 CHUNKS = len(CUTS) - 1
 EARLY = 2
 WIDE = BANDS * NEAR
@@ -191,9 +191,8 @@
     ]
     for load in loads:
         load.start()
-    for load in loads[:3]:
+    for load in loads[:2]:
         load.wait()
-    star_means(m_ref, w_ref, mean)
 
     @pl.when(is_home & moves)
     def _():
@@ -255,15 +254,17 @@
 
     teller = 0
 
+    @pl.when(moves)
+    def _():
+        for i in range(2):
+            ship_copy(i, band, 0).start()
+
+    loads[2].wait()
+    star_means(m_ref, w_ref, mean)
     for i in range(BANDS - 1):
         mate_copy(i).start()
     keep = pltpu.make_async_copy(mean, mates.at[band], local.at[4])
     keep.start()
-
-    @pl.when(moves)
-    def _():
-        for i in range(2):
-            ship_copy(i, band, 0).start()
 
     for load in loads[3:]:
         load.wait()

time: 105 us -> 105 us (level)
  no operation moved by 1% of the time
where the time goes in v7:
time: 105 us
  Pallas kernels  104 us (99%)
    pallas_call x1, Pallas kernels, solve(): pl.pallas_call(solve_kernel, out_shape=pltpu.VMEM((8, 512), F32), in_spec...  103 us

profile of v7, /device:TPU:1, one launch (start us, length us, event | category | flops | bytes accessed | tf_op | source)
XLA Modules:
  0.0 104.5 jit_solution(5083202815396076535)
XLA Ops:
  0.6 103.3 %solve.1.out_ref = f32[8,512]{1,0:T(8,128)S(1)} custom-call(f32[4,4]{1,0:T(4,128)} %ct_hbm.1, f32[8,2048]{1,0:T(8,128)} %bitcast.6, f32[8,2048]{1,0:T(8,128)} %bitcast.7, s32[8,2048]{1,0:T(8,128)} %bitcast.8, s32[32,128]{1,0:T(8,128)} %bitcast.9, s32[32,128]{1,0:T(8,128)} %bitcast.10, s32[8,32]{1,0:T(8,128)} %lst_hbm.1), custom_call_target="tpu_custom_call" | custom-call | tf_op jit(solution)/shard_map/solve/pallas_call | solution.py:735
  103.9 0.6 unpack.1

commit v8 on v7

--- a/solution.py
+++ b/solution.py
@@ -594,11 +594,12 @@
         zero = jnp.zeros((1, 128), F32)
         z = [jnp.where(colors[q] == 0.0, known[q] * scale[q], zero) for q in range(6)]
         cols = {q: columns(z[q]) for q in range(6)}
-        accs = pull([jnp.zeros((8, 128), F32) for _ in range(6)], range(6), cols)
-        for q in range(6):
-            out_buf[1, q] = jnp.sum(accs[q], axis=0, keepdims=True)
-        for slot in (2, 3, 0, 1):
-            step_copy(slot, 1).start()
+        for pieces, slots in ((outer, (2, 3)), (inner, (0, 1))):
+            accs = pull([jnp.zeros((8, 128), F32) for _ in pieces], pieces, cols)
+            for j, q in enumerate(pieces):
+                out_buf[1, q] = jnp.sum(accs[j], axis=0, keepdims=True)
+            for slot in slots:
+                step_copy(slot, 1).start()
         row_buf[0] = zero
 
         def renew(q, color, pulled, old):

time: 105 us -> 105 us (level)
  no operation moved by 1% of the time
where the time goes in v8:
time: 105 us
  Pallas kernels  104 us (99%)
    pallas_call x1, Pallas kernels, solve(): pl.pallas_call(solve_kernel, out_shape=pltpu.VMEM((8, 512), F32), in_spec...  103 us

profile of v8, /device:TPU:1, one launch (start us, length us, event | category | flops | bytes accessed | tf_op | source)
XLA Modules:
  0.0 104.5 jit_solution(7064157663067936948)
XLA Ops:
  0.6 103.3 %solve.1.out_ref = f32[8,512]{1,0:T(8,128)S(1)} custom-call(f32[4,4]{1,0:T(4,128)} %ct_hbm.1, f32[8,2048]{1,0:T(8,128)} %bitcast.6, f32[8,2048]{1,0:T(8,128)} %bitcast.7, s32[8,2048]{1,0:T(8,128)} %bitcast.8, s32[32,128]{1,0:T(8,128)} %bitcast.9, s32[32,128]{1,0:T(8,128)} %bitcast.10, s32[8,32]{1,0:T(8,128)} %lst_hbm.1), custom_call_target="tpu_custom_call" | custom-call | tf_op jit(solution)/shard_map/solve/pallas_call | solution.py:736
  103.9 0.6 unpack.1

commit v9 on v8

--- a/solution.py
+++ b/solution.py
@@ -511,12 +511,6 @@
                 fin[b, :, 0:ROWS] = means[b]
                 fin[b, 0:1, 256:384] = z[2 + b // 2]
                 fin[b, 1:8, 256:384] = jnp.zeros((7, 128), F32)
-            for slot in range(BANDS):
-
-                @pl.when(jnp.logical_not(owns(slot)))
-                def _():
-                    fin_copy(slot).start()
-
         lane = iota((1, 128), 1)
         found = jnp.zeros((1, 128), F32)
         for b in range(BANDS):
@@ -671,6 +665,12 @@
             plane_copy(i).start()
         mine = pltpu.make_async_copy(row_buf.at[0], plane.at[x * 4 + y], plane_recv)
         mine.start()
+        for slot in range(BANDS):
+
+            @pl.when(jnp.logical_not(owns(slot)))
+            def _():
+                fin_copy(slot).start()
+
         whole(plane, plane_recv).wait()
         row_buf[1] = jnp.sum(plane[...].reshape(16, 128), axis=0, keepdims=True)
         for i in range(len(LINE)):

time: 105 us -> 105 us (level)
  no operation moved by 1% of the time
where the time goes in v9:
time: 105 us; the launch traced here: 104 us
  Pallas kernels  104 us (99%)
    pallas_call x1, Pallas kernels, solve(): pl.pallas_call(solve_kernel, out_shape=pltpu.VMEM((8, 512), F32), in_spec...  103 us

profile of v9, /device:TPU:1, one launch (start us, length us, event | category | flops | bytes accessed | tf_op | source)
XLA Modules:
  0.0 104.5 jit_solution(6446248374768116757)
XLA Ops:
  0.6 103.2 %solve.1.out_ref = f32[8,512]{1,0:T(8,128)S(1)} custom-call(f32[4,4]{1,0:T(4,128)} %ct_hbm.1, f32[8,2048]{1,0:T(8,128)} %bitcast.6, f32[8,2048]{1,0:T(8,128)} %bitcast.7, s32[8,2048]{1,0:T(8,128)} %bitcast.8, s32[32,128]{1,0:T(8,128)} %bitcast.9, s32[32,128]{1,0:T(8,128)} %bitcast.10, s32[8,32]{1,0:T(8,128)} %lst_hbm.1), custom_call_target="tpu_custom_call" | custom-call | tf_op jit(solution)/shard_map/solve/pallas_call | solution.py:736
  103.9 0.6 unpack.1
